TPU v7x, 128 devices: a whole 4x4x4 slice. The times are simulated.
128 devices in a mesh: seq: 32 (over z, x, core), head: 4 (over y).
Axes of the slice: x: 4, y: 4, z: 4, core: 2. Of those that a mesh axis runs over, the one named last changes fastest.
Arguments:
- queries: bfloat16 [32768, 4096], P('seq', 'head'), may hold values from -8 to 8
- key_rows: bfloat16 [32768, 4096], P('seq', 'head'), may hold values from -8 to 8
- value_rows: bfloat16 [32768, 4096], P('seq', 'head'), may hold values from -6 to 6
- random_owner: int32 [512, 3], P('seq'), may hold values from 0 to 31, all different within a row; in each aligned block of 16 rows (0 to 15, 16 to 31, ...) at most 2 rows name the same one
- random_local: int32 [512, 3], P('seq'), may hold values from 0 to 15
- output_weight: bfloat16 [4096, 4096], P('head'), may hold values from -0.09375 to 0.09375
Outputs:
- layer_output: bfloat16 [32768, 4096], P(('seq', 'head'))
Inputs may be any that keep to these rules, and one draw needn't show every extreme that they name: `random_owner`: each row names 3 different owners. Among the rows of one device (16 aligned rows) no owner is named more than 2 times, and in some device's rows one owner is named exactly 2 times.
All inputs are finite; a program needn't handle non-finite values.
Results may differ from a plain program's by a relative error of at most 0.0052.
Values may be sent and summed in bfloat16 or wider, within the bound.
A program may use at most 192 MiB of HBM per device.

v0:
```python
import math

import jax
import jax.numpy as jnp
from jax import lax
from jax.sharding import Mesh
from jax.sharding import PartitionSpec as P

HEAD_DIM = 128
BLOCK = 64
RANDOM = 3
GLOBAL = 128
SEQ = ("seq_0", "seq_1", "seq_2")
SEQ_HEAD = ("seq_0", "seq_1", "seq_2", "head")


masked_score = -1e30


def padded(array, sides, width):
    for axis, dim in sides:
        peers, length = (lax.axis_size(axis), array.shape[dim])
        up = [(i, (i + 1) % peers) for i in range(peers - 1)]
        down = [(j, i) for i, j in up]
        last = lax.slice_in_dim(array, length - width, length, axis=dim)
        first = lax.slice_in_dim(array, 0, width, axis=dim)
        before = lax.ppermute(last, axis, up)
        after = lax.ppermute(first, axis, down)
        array = jnp.concatenate([before, array, after], axis=dim)
    return array


def broadcast(array, axis, root):
    return lax.dynamic_index_in_dim(lax.all_gather(array, axis), root, 0, keepdims=False)


def combined_by_axis(array, axes, combine):
    for axis in axes:
        pieces = jax.tree.map(lambda part: lax.all_gather(part, axis), array)
        array = jax.tree.map(lambda part: part[0], pieces)
        for k in range(1, lax.axis_size(axis)):
            array = combine(array, jax.tree.map(lambda part: part[k], pieces))
    return array


def slot_table(owner_ids, local_ids, seq_count, slot_count):
    owner_hits = (owner_ids[:, None] == jnp.arange(seq_count, dtype=jnp.int32)[None, :]).astype(
        jnp.int32
    )
    earlier = jnp.cumsum(owner_hits, axis=0) - owner_hits
    slot_ids = jnp.sum(earlier * owner_hits, axis=1)
    slot_hits = (slot_ids[:, None] == jnp.arange(slot_count, dtype=jnp.int32)[None, :]).astype(
        jnp.int32
    )
    request_table = jnp.sum(
        (owner_hits * local_ids[:, None])[:, :, None] * slot_hits[:, None, :], axis=0
    )
    return (request_table, slot_ids)


def local(queries, key_rows, value_rows, random_owner, random_local, output_weight):
    seq_count = lax.axis_size(SEQ)
    seq_index = lax.axis_index(SEQ)
    token_count, width_here = queries.shape
    blocks_here = token_count // BLOCK
    heads_here = width_here // HEAD_DIM
    slot_count = max(2, 4 * blocks_here // seq_count)
    total_blocks = seq_count * blocks_here
    score_scale = HEAD_DIM ** (-0.5)
    key_blocks = key_rows.reshape(blocks_here, BLOCK, width_here)
    value_blocks = value_rows.reshape(blocks_here, BLOCK, width_here)
    edge_slots = 0
    owner_flat = random_owner.reshape(-1)
    local_flat = random_local.reshape(-1)
    request_table, slot_ids = slot_table(owner_flat, local_flat, seq_count, slot_count)
    wanted = lax.all_to_all(request_table, SEQ, split_axis=0, concat_axis=0, tiled=True)
    sent_keys = jnp.take(key_blocks, wanted, axis=0)
    sent_values = jnp.take(value_blocks, wanted, axis=0)
    got_keys = lax.all_to_all(sent_keys, SEQ, split_axis=0, concat_axis=0, tiled=True)
    got_values = lax.all_to_all(sent_values, SEQ, split_axis=0, concat_axis=0, tiled=True)
    slot_width = slot_count + edge_slots
    flat_slots = owner_flat * slot_width + slot_ids
    random_keys = jnp.take(got_keys.reshape(-1, BLOCK, width_here), flat_slots, axis=0)
    random_values = jnp.take(got_values.reshape(-1, BLOCK, width_here), flat_slots, axis=0)
    edge_pairs = jnp.stack(
        [jnp.stack([key_blocks[0], value_blocks[0]]), jnp.stack([key_blocks[-1], value_blocks[-1]])]
    )
    widened = padded(edge_pairs, ((SEQ, 0),), 1)
    left_key, left_value = (widened[0, 0], widened[0, 1])
    right_key, right_value = (widened[3, 0], widened[3, 1])
    global_rows = jnp.stack([queries[:GLOBAL], key_rows[:GLOBAL], value_rows[:GLOBAL]])
    global_rows = broadcast(global_rows, SEQ, 0)
    global_query = global_rows[0].reshape(GLOBAL, heads_here, HEAD_DIM)
    key_heads = key_rows.reshape(token_count, heads_here, HEAD_DIM)
    value_heads = value_rows.reshape(token_count, heads_here, HEAD_DIM)
    scores = (
        jnp.einsum("qhd,khd->hqk", global_query, key_heads, preferred_element_type=jnp.float32)
        * score_scale
    )
    row_max = jnp.max(scores, axis=2)
    weight = jnp.exp(scores - row_max[:, :, None])
    row_total = jnp.sum(weight, axis=2)
    partial_value = jnp.einsum(
        "hqk,khd->hqd", weight.astype(jnp.bfloat16), value_heads, preferred_element_type=jnp.float32
    )

    def combine(left_part, right_part):
        joint_max = jnp.maximum(left_part[0], right_part[0])
        left_factor = jnp.exp(left_part[0] - joint_max)
        right_factor = jnp.exp(right_part[0] - joint_max)
        return (
            joint_max,
            left_part[1] * left_factor + right_part[1] * right_factor,
            left_part[2] * left_factor[:, :, None] + right_part[2] * right_factor[:, :, None],
        )

    row_max, row_total, partial_value = combined_by_axis(
        (row_max, row_total, partial_value), SEQ, combine
    )
    global_out = jnp.transpose(partial_value / row_total[:, :, None], (1, 0, 2)).reshape(
        GLOBAL, width_here
    )
    key_padded = jnp.concatenate([left_key[None], key_blocks, right_key[None]], axis=0)
    value_padded = jnp.concatenate([left_value[None], value_blocks, right_value[None]], axis=0)
    global_keys = global_rows[1].reshape(GLOBAL // BLOCK, BLOCK, width_here)
    global_values = global_rows[2].reshape(GLOBAL // BLOCK, BLOCK, width_here)
    group_size = math.gcd(blocks_here, max(1, 512 // BLOCK))
    group_count = blocks_here // group_size
    listed = (3 + RANDOM) * BLOCK + GLOBAL
    slot_number = jnp.arange(listed, dtype=jnp.int32) // BLOCK

    def attend(packed):
        number, query_group, key_group, value_group = packed
        block_ids = (
            seq_index * blocks_here + number * group_size + jnp.arange(group_size, dtype=jnp.int32)
        )
        near_keys = lax.dynamic_slice_in_dim(key_padded, number * group_size, group_size + 2, 0)
        near_values = lax.dynamic_slice_in_dim(value_padded, number * group_size, group_size + 2, 0)
        window_keys = jnp.stack([near_keys[:-2], near_keys[1:-1], near_keys[2:]], axis=1)
        window_values = jnp.stack([near_values[:-2], near_values[1:-1], near_values[2:]], axis=1)
        listed_keys = jnp.concatenate(
            [
                window_keys,
                key_group,
                jnp.broadcast_to(global_keys[None], (group_size,) + global_keys.shape),
            ],
            axis=1,
        )
        listed_values = jnp.concatenate(
            [
                window_values,
                value_group,
                jnp.broadcast_to(global_values[None], (group_size,) + global_values.shape),
            ],
            axis=1,
        )
        group_keys = listed_keys.reshape(group_size, listed, heads_here, HEAD_DIM)
        group_values = listed_values.reshape(group_size, listed, heads_here, HEAD_DIM)
        query_heads = query_group.reshape(group_size, BLOCK, heads_here, HEAD_DIM)
        block_scores = (
            jnp.einsum(
                "bqhd,bkhd->bhqk", query_heads, group_keys, preferred_element_type=jnp.float32
            )
            * score_scale
        )
        usable = jnp.logical_and(
            jnp.logical_or(slot_number[None, :] != 0, block_ids[:, None] > 0),
            jnp.logical_or(slot_number[None, :] != 2, block_ids[:, None] < total_blocks - 1),
        )
        usable_keys = usable[:, None, None, :]
        block_scores = jnp.where(usable_keys, block_scores, masked_score)
        block_max = jnp.max(block_scores, axis=3, keepdims=True)
        block_weight = jnp.where(usable_keys, jnp.exp(block_scores - block_max), 0.0)
        block_total = jnp.sum(block_weight, axis=3)
        context = jnp.einsum(
            "bhqk,bkhd->bqhd",
            block_weight.astype(jnp.bfloat16),
            group_values,
            preferred_element_type=jnp.float32,
        )
        context = context / jnp.transpose(block_total, (0, 2, 1))[:, :, :, None]
        return context.reshape(group_size * BLOCK, width_here).astype(jnp.bfloat16)

    numbers = jnp.arange(group_count, dtype=jnp.int32)
    query_groups = queries.reshape(group_count, group_size, BLOCK, width_here)
    random_key_groups = random_keys.reshape(group_count, group_size, RANDOM, BLOCK, width_here)
    random_value_groups = random_values.reshape(group_count, group_size, RANDOM, BLOCK, width_here)
    sparse = lax.map(
        attend, (numbers, query_groups, random_key_groups, random_value_groups)
    ).reshape(token_count, width_here)
    top_rows = jnp.where(seq_index == 0, global_out.astype(jnp.bfloat16), sparse[:GLOBAL])
    attention = jnp.concatenate([top_rows, sparse[GLOBAL:]], axis=0)
    summed = lax.psum_scatter(
        jnp.dot(attention, output_weight, preferred_element_type=jnp.float32),
        "head",
        scatter_dimension=0,
        tiled=True,
    )
    return summed.astype(jnp.bfloat16)


def solution(mesh):
    split = Mesh(
        mesh.devices.reshape(4, 4, 2, mesh.shape["head"]), ("seq_0", "seq_1", "seq_2", "head")
    )
    placed = (
        P(SEQ, "head"),
        P(SEQ, "head"),
        P(SEQ, "head"),
        P(SEQ, None),
        P(SEQ, None),
        P("head", None),
    )
    return jax.shard_map(
        local, mesh=split, in_specs=placed, out_specs=P(SEQ_HEAD, None), check_vma=False
    )
```

profile of v0, /device:TPU:1, one launch (start us, length us, event | category | flops | bytes accessed | tf_op | source)
XLA Modules:
  0.0 730.8 jit_solution(16248240682191572009)
XLA Ops:
  11.9 16.3 %all_to_all.22 = s32[32,1,2]{2,1,0:T(1,128)S(1)} all-to-all(s32[32,1,2]{2,1,0:T(1,128)S(1)} %copy.91), channel_id=1, replica_groups=mesh['seq_0'=4,'seq_1'=4,'seq_2'=2,'head'=4] {'seq_0','seq_1','seq_2'}, dimensions={0} | all-to-all | bytes 512 | tf_op jit(solution)/shard_map/all_to_all | solution.py:76
  28.5 7.4 %gather_fusion = bf16[64,64,1024]{2,1,0:T(8,128)(2,1)} fusion(bf16[16,64,1024]{2,1,0:T(8,128)(2,1)} %bitcast.364, s32[1024]{0:T(1024)S(1)} %pad_clamp_fusion.1), kind=kCustom, calls=%fused_computation.clone | custom fusion | bytes 16777472 | tf_op jit(solution)/shard_map/jit(_take)/gather | solution.py:78
  41.5 9.8 %broadcast_select_fusion = (bf16[32,2,64,1024]{3,2,1,0:T(8,128)(2,1)}, bf16[32,2,64,1024]{3,2,1,0:T(8,128)(2,1)S(1)}) fusion(bf16[32,2,64,1024]{3,2,1,0:T(8,128)(2,1)} %bitcast.367, pred[32,2]{1,0:T(8,128)(4,1)S(1)} %copy.93, bf16[32,2,64,1024]{3,2,1,0:T(8,128)(2,1)} %bitcast.366), kind=kLoop, calls=%fused_computation.53 | loop fusion | flops 8388608 | bytes 33554496 | tf_op jit(solution)/shard_map/jit(_take)/select_n | solution.py:77
  51.3 142.6 %all_to_all.23 = bf16[32,2,64,1024]{3,2,1,0:T(8,128)(2,1)} all-to-all(bf16[32,2,64,1024]{3,2,1,0:T(8,128)(2,1)S(1)} %get-tuple-element.301), channel_id=1, replica_groups=mesh['seq_0'=4,'seq_1'=4,'seq_2'=2,'head'=4] {'seq_0','seq_1','seq_2'}, dimensions={0} | all-to-all | bytes 16777216 | tf_op jit(solution)/shard_map/all_to_all | solution.py:80
  200.1 29.5 %copy.82 = bf16[96,128,1024]{1,2,0:T(8,128)(2,1)} copy(bf16[96,128,1024]{2,1,0:T(8,128)(2,1)} %all-gather.13.cloned.1.call-done) | data formatting | bytes 50331648 | tf_op jit(solution)/shard_map/all_gather | solution.py:34
  240.5 73.2 %all-gather.2 = f32[32,128]{1,0:T(8,128)S(1)} all-gather(f32[8,128]{1,0:T(8,128)S(1)} %get-tuple-element.306), channel_id=4, replica_groups=mesh['seq_0'=4,'seq_1'=4,'seq_2'=2,'head'=4] {'seq_0'}, dimensions={0}, use_global_device_ids=true | all-gather | bytes 20480 | tf_op jit(solution)/shard_map/all_gather | solution.py:39
  328.2 8.4 %gather_fusion.1 = bf16[48,64,1024]{2,1,0:T(8,128)(2,1)} fusion(bf16[64,64,1024]{2,1,0:T(8,128)(2,1)} %bitcast.369, s32[1024]{0:T(1024)S(1)} %pad_clamp_fusion), kind=kCustom, calls=%fused_computation.1.clone | custom fusion | bytes 12583104 | tf_op jit(solution)/shard_map/jit(_take)/gather | solution.py:84
  336.6 8.5 %gather_fusion.3 = bf16[48,64,1024]{2,1,0:T(8,128)(2,1)} fusion(bf16[64,64,1024]{2,1,0:T(8,128)(2,1)} %bitcast.49, s32[1024]{0:T(1024)S(1)} %pad_clamp_fusion), kind=kCustom, calls=%fused_computation.3.clone | custom fusion | bytes 12583104 | tf_op jit(solution)/shard_map/jit(_take)/gather | solution.py:83
  345.1 10.4 %broadcast_select_fusion.2 = (bf16[48,64,1024]{2,1,0:T(8,128)(2,1)}, bf16[48,64,1024]{2,1,0:T(8,128)(2,1)}) fusion(bf16[48,64,1024]{2,1,0:T(8,128)(2,1)} %gather_fusion.3, pred[48]{0:T(512)(128)(4,1)S(1)} %get-tuple-element.267, bf16[48,64,1024]{2,1,0:T(8,128)(2,1)} %gather_fusion.1), kind=kLoop, calls=%fused_computation.55 | loop fusion | flops 6291456 | bytes 25165872 | tf_op jit(solution)/shard_map/jit(_take)/select_n | solution.py:83
  360.2 9.1 %all-gather.3 = f32[32,128]{1,0:T(8,128)S(1)} all-gather(f32[8,128]{1,0:T(8,128)S(1)} %fusion.33), channel_id=5, replica_groups=mesh['seq_0'=4,'seq_1'=4,'seq_2'=2,'head'=4] {'seq_0'}, dimensions={0}, use_global_device_ids=true | all-gather | bytes 20480 | tf_op jit(solution)/shard_map/all_gather | solution.py:39
  370.0 10.0 %all_gather.55 = f32[4,8,128]{2,1,0:T(8,128)S(1)} all-gather(f32[1,8,128]{2,1,0:T(8,128)S(1)} %get-tuple-element.262), channel_id=1, replica_groups=mesh['seq_0'=4,'seq_1'=4,'seq_2'=2,'head'=4] {'seq_1'}, dimensions={0}, use_global_device_ids=true | all-gather | bytes 20480 | tf_op jit(solution)/shard_map/all_gather | solution.py:39
  383.6 147.3 %while.14 = (s32[]{:T(128)}, bf16[2,512,1024]{2,1,0:T(8,128)(2,1)}, s32[2]{0:T(128)S(1)}, bf16[18,64,1024]{2,1,0:T(8,128)(2,1)S(1)}, bf16[2,8,3,64,1024]{4,3,2,1...) while((s32[]{:T(128)}, bf16[2,512,1024]{2,1,0:T(8,128)(2,1)}, ...), condition=%wide.region_8.11_spmd.clone.clone, body=%wide.region_5.10_spmd.clone.clone.sunk | while | flops 1091585536 | bytes 126397792 | solution.py:188
  404.6 8.9 %copy.140 = bf16[512,8,8,128]{3,2,1,0:T(8,128)(2,1)} copy(bf16[512,8,8,128]{3,1,2,0:T(8,128)(2,1)} %bitcast.350) | data formatting | bytes 16777216 | tf_op jit(solution)/shard_map/while
  413.9 9.7 %fusion.136 = f32[8,8,64,512]{3,2,1,0:T(8,128)} fusion(bf16[8,512,8,128]{3,2,1,0:T(8,128)(2,1)} %bitcast.355, bf16[8,64,8,128]{3,2,1,0:T(8,128)(2,1)S(1)} %bitcast.358), kind=kOutput, calls=%fused_computation.8.clone.1 | convolution fusion | flops 536870912 | bytes 17825792 | tf_op jit(solution)/shard_map/while/body/eval_jaxpr/bqhd,bkhd->bhqk/dot_general | solution.py:161
  423.7 11.5 %fusion.139 = (f32[8,8,64]{2,1,0:T(8,128)S(1)}, bf16[8,8,64,512]{3,2,1,0:T(8,128)(2,1)}) fusion(f32[8,8,64,512]{3,2,1,0:T(8,128)} %fusion.136, pred[8,512]{1,0:T(8,128)(4,1)S(1)} %or_and_fusion.2), kind=kOutput, calls=%fused_computation.205.clone.1 | output fusion | flops 16777728 | bytes 12603392 | tf_op jit(solution)/shard_map/while/body/eval_jaxpr/sub | solution.py:173
  437.8 8.8 %copy.139 = bf16[512,8,8,128]{3,2,1,0:T(8,128)(2,1)} copy(bf16[512,8,8,128]{3,1,2,0:T(8,128)(2,1)} %bitcast.356) | data formatting | bytes 16777216 | tf_op jit(solution)/shard_map/while
  478.0 8.9 %copy.140 = bf16[512,8,8,128]{3,2,1,0:T(8,128)(2,1)} copy(bf16[512,8,8,128]{3,1,2,0:T(8,128)(2,1)} %bitcast.350) | data formatting | bytes 16777216 | tf_op jit(solution)/shard_map/while
  487.3 9.7 %fusion.136 = f32[8,8,64,512]{3,2,1,0:T(8,128)} fusion(bf16[8,512,8,128]{3,2,1,0:T(8,128)(2,1)} %bitcast.355, bf16[8,64,8,128]{3,2,1,0:T(8,128)(2,1)S(1)} %bitcast.358), kind=kOutput, calls=%fused_computation.8.clone.1 | convolution fusion | flops 536870912 | bytes 17825792 | tf_op jit(solution)/shard_map/while/body/eval_jaxpr/bqhd,bkhd->bhqk/dot_general | solution.py:161
  497.1 11.5 %fusion.139 = (f32[8,8,64]{2,1,0:T(8,128)S(1)}, bf16[8,8,64,512]{3,2,1,0:T(8,128)(2,1)}) fusion(f32[8,8,64,512]{3,2,1,0:T(8,128)} %fusion.136, pred[8,512]{1,0:T(8,128)(4,1)S(1)} %or_and_fusion.2), kind=kOutput, calls=%fused_computation.205.clone.1 | output fusion | flops 16777728 | bytes 12603392 | tf_op jit(solution)/shard_map/while/body/eval_jaxpr/sub | solution.py:173
  511.2 8.8 %copy.139 = bf16[512,8,8,128]{3,2,1,0:T(8,128)(2,1)} copy(bf16[512,8,8,128]{3,1,2,0:T(8,128)(2,1)} %bitcast.356) | data formatting | bytes 16777216 | tf_op jit(solution)/shard_map/while
  536.9 9.2 %all_gather.60 = f32[4,8,128]{2,1,0:T(8,128)S(1)} all-gather(f32[1,8,128]{2,1,0:T(8,128)S(1)} %copy-done.8), channel_id=1, replica_groups=mesh['seq_0'=4,'seq_1'=4,'seq_2'=2,'head'=4] {'seq_1'}, dimensions={0}, use_global_device_ids=true | all-gather | bytes 20480 | tf_op jit(solution)/shard_map/all_gather | solution.py:39
  546.1 9.2 %all_gather.57 = f32[2,8,128]{2,1,0:T(8,128)S(1)} all-gather(f32[1,8,128]{2,1,0:T(8,128)S(1)} %get-tuple-element.260), channel_id=1, replica_groups=mesh['seq_0'=4,'seq_1'=4,'seq_2'=2,'head'=4] {'seq_2'}, dimensions={0}, use_global_device_ids=true | all-gather | bytes 12288 | tf_op jit(solution)/shard_map/all_gather | solution.py:39
  560.0 14.6 %fusion.42 = f32[1024,4096]{1,0:T(8,128)} fusion(bf16[1024,4096]{1,0:T(8,128)(2,1)} %param.17, bf16[896,1024]{0,1:T(8,128)(2,1)S(1)} %copy-done.5, bf16[128,1024]{0,1:T(8,128)(2,1)S(1)} %bitcast_select_fusion), kind=kOutput, calls=%fused_computation.69 | convolution fusion | flops 8594128896 | bytes 27262976 | tf_op jit(solution)/shard_map/dot_general | solution.py:194
  574.5 146.0 %reduce-scatter.2.cloned.1.call-done = f32[256,4096]{1,0:T(8,128)} async-done(((f32[1024,4096]{1,0:T(8,128)}), f32[256,4096]{1,0:T(8,128)}) %reduce-scatter.2.cloned.1.call-update) | async-done | bytes 4194320 | tf_op jit(solution)/shard_map/reduce_scatter | solution.py:193
  (138 shorter events, 133.9 us)
Async XLA Ops:
  6.5 193.5 %all-gather.13.cloned.1.call-start = ((), (), s32[]{:S(2)}) async-start(), calls=%async_computation.7 | async-start | bytes 25952256 | tf_op jit(solution)/shard_map/all_gather | solution.py:34
  28.5 7.4 %copy-start = (bf16[1024,1024]{1,0:T(8,128)(2,1)S(1)}, bf16[1024,1024]{1,0:T(8,128)(2,1)}, u32[]{:S(2)}) copy-start(bf16[1024,1024]{1,0:T(8,128)(2,1)} %param.13) | copy-start | bytes 6291460
  194.0 142.6 %all-to-all-start.2 = ((bf16[32,2,64,1024]{3,2,1,0:T(8,128)(2,1)}), bf16[32,2,64,1024]{3,2,1,0:T(8,128)(2,1)}, u32[]{:S(2)}, u32[]{:S(2)}) async-start(bf16[32,2,64,1024]{3,2,1,0:T(8,128)(2,1)} %get-tuple-element.300), calls=%async_computation.2 | async-start | bytes 16777216 | tf_op jit(solution)/shard_map/all_to_all | solution.py:79
  200.0 113.7 %all-gather.15.cloned.1.call-start = ((), (), s32[]{:S(2)}) async-start(), calls=%async_computation.8 | async-start | bytes 2621440 | tf_op jit(solution)/shard_map/all_gather | solution.py:39
  229.6 4.2 copy-start.2
  231.8 2.0 copy-start.3
  235.9 144.8 %all-gather.9.cloned.1.call-start = ((), (), s32[]{:S(2)}) async-start(), calls=%async_computation.4 | async-start | bytes 2621440 | tf_op jit(solution)/shard_map/all_gather | solution.py:39
  237.0 85.4 %collective-permute-start = (bf16[1,2,64,1024]{3,2,1,0:T(8,128)(2,1)S(1)}, bf16[1,2,64,1024]{3,2,1,0:T(8,128)(2,1)S(1)}, u32[]{:S(2)}, u32[]{:S(2)}) collective-permute-start(bf16[1,2,64,1024]{3,2,1,0:T(8,128)(2,1)S(1)} %maximum_bitcast_fusion), channel_id=1, source_target_pairs={{0,4},{4,8},{8,12},{12,16},{16,20},{20,24},{24,28},{28,32},{32,36}... | collective-permute-start | bytes 786440 | tf_op jit(solution)/shard_map/ppermute | solution.py:27
  316.6 240.5 %all-gather.11.cloned.1.call-start = ((), (), s32[]{:S(2)}) async-start(), calls=%async_computation.5 | async-start | bytes 1572864 | tf_op jit(solution)/shard_map/all_gather | solution.py:39
  316.7 7.7 %collective-permute-start.1 = (bf16[1,2,64,1024]{3,2,1,0:T(8,128)(2,1)S(1)}, bf16[1,2,64,1024]{3,2,1,0:T(8,128)(2,1)S(1)}, u32[]{:S(2)}, u32[]{:S(2)}) collective-permute-start(bf16[1,2,64,1024]{3,2,1,0:T(8,128)(2,1)S(1)} %maximum_bitcast_fusion.1), channel_id=1, source_target_pairs={{4,0},{8,4},{12,8},{16,12},{20,16},{24,20},{28,24},{32,28},{36,32}... | collective-permute-start | bytes 786440 | tf_op jit(solution)/shard_map/ppermute | solution.py:28
  322.3 4.1 copy-start.1
  380.0 0.6 copy-start.6
  383.6 337.0 %reduce-scatter.2.cloned.1.call-start = ((), (), s32[]{:S(2)}) async-start(), calls=%async_computation.6 | async-start | bytes 20971520 | tf_op jit(solution)/shard_map/reduce_scatter | solution.py:193
  404.6 8.9 %copy-start.4 = (bf16[2,8,64,1024]{3,2,1,0:T(8,128)(2,1)S(1)}, bf16[2,8,64,1024]{3,2,1,0:T(8,128)(2,1)}, u32[]{:S(2)}) copy-start(bf16[2,8,64,1024]{3,2,1,0:T(8,128)(2,1)} %get-tuple-element.436) | copy-start | bytes 6291460 | tf_op jit(solution)/shard_map/while
  478.0 8.9 %copy-start.4 = (bf16[2,8,64,1024]{3,2,1,0:T(8,128)(2,1)S(1)}, bf16[2,8,64,1024]{3,2,1,0:T(8,128)(2,1)}, u32[]{:S(2)}) copy-start(bf16[2,8,64,1024]{3,2,1,0:T(8,128)(2,1)} %get-tuple-element.436) | copy-start | bytes 6291460 | tf_op jit(solution)/shard_map/while
  530.9 5.9 copy-start.8
  530.9 15.2 %copy-start.7 = (f32[4,8,128]{2,1,0:T(8,128)S(1)}, f32[4,8,128]{2,1,0:T(8,128)}, u32[]{:S(2)}) copy-start(f32[4,8,128]{2,1,0:T(8,128)} %copy-done.6) | copy-start | bytes 49156
  536.9 23.1 %copy-start.5 = (bf16[896,1024]{0,1:T(8,128)(2,1)S(1)}, bf16[896,1024]{0,1:T(8,128)(2,1)}, u32[]{:S(2)}) copy-start(bf16[896,1024]{0,1:T(8,128)(2,1)} %copy.105) | copy-start | bytes 5505028
Sparse Core Ops, SparseCore 0:
  9.7 183.1 all-gather.12
  236.0 76.0 all-gather.14
  316.8 30.5 all-gather.8
  383.7 14.9 all-gather.10
  574.7 145.8 reduce-scatter.1
where the time goes:
time: 733 us; the launch traced here: 731 us
  blocking collectives  271 us (37%)
  local copies, waits for them, and re-layouts  168 us (23%)
  waiting for transfers between devices  148 us (20%)
  other arithmetic  63 us (9%)
  matrix products  50.1 us (7%)
  starting transfers between devices  15.3 us (2%)
  between operations  13.4 us (2%)
    reduce_scatter x1, waiting for transfers between devices, local(): lax.psum_scatter(jnp.dot(attention, output_weight, preferred_element_type...  146 us
    all_to_all x1, blocking collectives, local(): lax.all_to_all(sent_values, SEQ, split_axis=0, concat_axis=0, tiled=True)  143 us
    all_gather x6, blocking collectives, combined_by_axis(): pieces = jax.tree.map(lambda part: lax.all_gather(part, axis), array)  113 us
    while x24, local copies, waits for them, and re-layouts  69.9 us
    all_gather x1, local copies, waits for them, and re-layouts, broadcast(): lax.all_gather(array, axis)  29.5 us
    sub x2, other arithmetic, attend(): block_scores - block_max  23 us
    dot_general x2, matrix products, attend(): jnp.einsum('bqhd,bkhd->bhqk', query_heads, group_keys, preferred_element_...  19.4 us
    all_to_all x1, blocking collectives, local(): lax.all_to_all(request_table, SEQ, split_axis=0, concat_axis=0, tiled=True)  16.3 us
  transfers between devices with their start and end apart: 8, of which 2 were waited for; matrix products, arithmetic and copies ran while one was open for 34% of the time, Pallas kernels for 0%

commit v1 on v0

v1 whole, which is shorter than its diff:
```python
import math

import jax
import jax.numpy as jnp
from jax import lax
from jax.experimental import pallas as pl
from jax.experimental.pallas import tpu as pltpu
from jax.sharding import PartitionSpec as P

MESH = pl.DeviceIdType.MESH
HD = 128
BLK = 64
GLOB = 128
ROWS = 1024
WIDTH = 1024
CHUNKS = 4
HPC = 2
CW = HPC * HD
SCALE2 = HD ** (-0.5) * math.log2(math.e)
BF = jnp.bfloat16
F32 = jnp.float32
NT = (((1,), (1,)), ((), ()))
TN = (((0,), (0,)), ((), ()))


def table_kernel(owner, place, reqk, reqv, kidx, vidx, count):
    def clear(i, carry):
        count[i] = 0
        return carry

    lax.fori_loop(0, 32, clear, 0)

    def blank(i, carry):
        reqk[i // 8, 0, i % 8] = 0
        reqv[i // 8, 0, i % 8] = 0
        return carry

    lax.fori_loop(0, 64, blank, 0)

    def fill(i, carry):
        o = owner[i // 3, i % 3]
        p = place[i // 3, i % 3]
        n = count[o]
        count[o] = n + 1
        z, x, c = o // 8, (o // 2) % 4, o % 2
        reqk[x * 2 + c, 0, z * 2 + n] = p
        reqv[z * 2 + c, 0, x * 2 + n] = p
        kidx[i] = (x * 2 + c) * 8 + z * 2 + n
        vidx[i] = (z * 2 + c) * 8 + x * 2 + n
        return carry

    lax.fori_loop(0, 48, fill, 0)


def tables(owner, place):
    smem = pl.BlockSpec(memory_space=pltpu.SMEM)
    i32 = jnp.int32
    return pl.pallas_call(
        table_kernel,
        out_shape=[
            jax.ShapeDtypeStruct((8, 1, 128), i32),
            jax.ShapeDtypeStruct((8, 1, 128), i32),
            jax.ShapeDtypeStruct((48,), i32),
            jax.ShapeDtypeStruct((48,), i32),
        ],
        in_specs=[smem, smem],
        out_specs=[smem] * 4,
        scratch_shapes=[pltpu.SMEM((32,), i32)],
        name="tables",
    )(owner, place)


def main_kernel(
    kidx, vidx, reqk, reqv, q_hbm, k_hbm, v_hbm, w_hbm,
    att_out, wfull,
    kag, vag, kx, vx, qv, stk, stv, rk0, rk1, rk2, rk3, rv0, rv1, rv2, rv3,
    gq, gk, gv, att, part, r1, r2, comb, gout, rqk, rqv, sqk, sqv,
    loc, rq_s, rq_r, ed_s, ed_r, ag_s, ag_r, w_s, w_r, wd_s, wd_r,
    a2_s, a2_r, g_s, g_r, y_s, y_r, r1_s, r1_r, r2_s, r2_r, r3_s, r3_r,
):
    rks, rvs = (rk0, rk1, rk2, rk3), (rv0, rv1, rv2, rv3)
    s = lax.axis_index("seq")
    y = lax.axis_index("head")
    z, x, c = s // 8, (s // 2) % 4, s % 2
    xc, zc = x * 2 + c, z * 2 + c

    def at(dz=0, dx=0, dc=0, dy=0):
        return ((((z + dz) % 4) * 4 + (x + dx) % 4) * 2 + (c + dc) % 2, (y + dy) % 4)

    def remote(src, dst, ss, rs, dev):
        return pltpu.make_async_remote_copy(
            src_ref=src, dst_ref=dst, send_sem=ss, recv_sem=rs, device_id=dev, device_id_type=MESH
        )

    nxt, prv = ((s + 1) % 32, y), ((s + 31) % 32, y)
    row_peers = [(dx, dc) for dx in (1, 3, 2, 0) for dc in (0, 1) if (dx, dc) != (0, 0)]

    own = [
        pltpu.make_async_copy(k_hbm, kag.at[z], loc.at[0]),
        pltpu.make_async_copy(v_hbm, vag.at[x], loc.at[1]),
        pltpu.make_async_copy(k_hbm, kx.at[pl.ds(1, 16)], loc.at[2]),
        pltpu.make_async_copy(v_hbm, vx.at[pl.ds(1, 16)], loc.at[3]),
        pltpu.make_async_copy(q_hbm, qv, loc.at[4]),
    ]
    for cp in own:
        cp.start()

    bar = pltpu.get_barrier_semaphore()
    peers = [at(dx=dx, dc=dc) for dx, dc in row_peers]
    peers += [at(dz=dz, dc=dc) for dz in (1, 2, 3) for dc in (0, 1)]
    peers += [at(dy=dy) for dy in (1, 2, 3)]
    peers += [nxt, prv]
    for dev in peers:
        pl.semaphore_signal(bar, inc=1, device_id=dev, device_id_type=MESH)
    root = jnp.logical_and(s == 0, y == 0)

    @pl.when(z == 0)
    def _():
        @pl.when(jnp.logical_not(root))
        def _():
            pl.semaphore_signal(bar, inc=1, device_id=(0, 0), device_id_type=MESH)

    @pl.when(root)
    def _():
        for ss in range(8):
            for yy in range(4):
                if (ss, yy) != (0, 0):
                    pl.semaphore_signal(bar, inc=1, device_id=(ss, yy), device_id_type=MESH)
        pl.semaphore_wait(bar, len(peers) + 31)

    @pl.when(jnp.logical_not(root))
    def _():
        @pl.when(z == 0)
        def _():
            pl.semaphore_wait(bar, len(peers) + 1)

        @pl.when(z != 0)
        def _():
            pl.semaphore_wait(bar, len(peers))

    late = []

    def go(cp):
        cp.start()
        late.append(cp)
        return cp

    rq = []
    for i, (dx, dc) in enumerate(row_peers):
        tgt = ((x + dx) % 4) * 2 + (c + dc) % 2
        rq.append(go(remote(reqk.at[tgt], rqk.at[xc], rq_s.at[0, i], rq_r.at[0, i], at(dx=dx, dc=dc))))
        tgt = ((z + dx) % 4) * 2 + (c + dc) % 2
        rq.append(go(remote(reqv.at[tgt], rqv.at[zc], rq_s.at[1, i], rq_r.at[1, i], at(dz=dx, dc=dc))))

    is00 = jnp.logical_and(x == 0, c == 0)

    def gcopy(src, dst, n, i, dev):
        return remote(src, dst, g_s.at[n, i], g_r.at[n], dev)

    q_top = q_hbm.at[pl.ds(0, GLOB)]
    q_root = pltpu.make_async_copy(q_top, gq, g_r.at[0])

    @pl.when(s == 0)
    def _():
        q_root.start()
        for dz in (1, 3, 2):
            gcopy(q_top, gq, 0, dz, at(dz=dz)).start()

    edges = []
    for i, (hbm, ext) in enumerate(((k_hbm, kx), (v_hbm, vx))):
        edges.append(go(remote(hbm.at[0], ext.at[17], ed_s.at[i, 0], ed_r.at[i, 0], prv)))
        edges.append(go(remote(hbm.at[15], ext.at[0], ed_s.at[i, 1], ed_r.at[i, 1], nxt)))

    def gather(n, own_view, view, up, down, me, ss, rs):
        a = go(remote(own_view(0), view(me, 0), ss.at[n, 0], rs.at[n, 0], up))
        b = go(remote(own_view(1), view(me, 1), ss.at[n, 1], rs.at[n, 1], down))
        d = go(remote(own_view(1), view(me, 1), ss.at[n, 2], rs.at[n, 2], up))
        e = go(remote(own_view(0), view(me, 0), ss.at[n, 3], rs.at[n, 3], down))
        before, after = (me + 3) % 4, (me + 1) % 4
        f = remote(view(before, 0), view(before, 0), ss.at[n, 4], rs.at[n, 4], up)
        g = remote(view(after, 1), view(after, 1), ss.at[n, 5], rs.at[n, 5], down)
        return a, b, d, e, f, g

    agk = gather(
        0, lambda p: k_hbm.at[pl.ds(p * 8, 8)],
        lambda m, p: kag.at[m, pl.ds(p * 8, 8)], at(dz=1), at(dz=3), z, ag_s, ag_r,
    )
    agv = gather(
        1, lambda p: v_hbm.at[pl.ds(p * 8, 8)],
        lambda m, p: vag.at[m, pl.ds(p * 8, 8)], at(dx=1), at(dx=3), x, ag_s, ag_r,
    )
    half = ROWS // 2
    wq = ROWS // 4

    def wview(m, p):
        return wfull.at[pl.ds(m * ROWS + c * half + p * wq, wq)]

    agw = gather(
        0, lambda p: w_hbm.at[pl.ds(c * half + p * wq, wq)],
        wview, at(dy=1), at(dy=3), y, w_s, w_r,
    )
    mate = at(dc=1)
    wown = go(remote(w_hbm, wfull.at[pl.ds(y * ROWS, ROWS)], wd_s.at[6], wd_r.at[6], mate))

    @pl.when(is00)
    def _():
        @pl.when(s == 0)
        def _():
            q_root.wait()

        @pl.when(s != 0)
        def _():
            gcopy(q_top, gq, 0, 0, at()).wait_recv()

        for dx in (1, 3, 2):
            gcopy(gq, gq, 1, dx, at(dx=dx)).start()

    @pl.when(c == 0)
    def _():
        @pl.when(x != 0)
        def _():
            gcopy(gq, gq, 1, 0, at()).wait_recv()

        gcopy(gq, gq, 2, 0, mate).start()

    @pl.when(c == 1)
    def _():
        gcopy(gq, gq, 2, 0, at()).wait_recv()

    for cp in own:
        cp.wait()

    for cp in rq:
        cp.wait_recv()
    rqk[xc] = reqk[xc]
    rqv[zc] = reqv[zc]
    to_s = [pltpu.make_async_copy(rqk, sqk, loc.at[5]), pltpu.make_async_copy(rqv, sqv, loc.at[6])]

    def glob(h, carry):
        cols = pl.ds(pl.multiple_of(h * HD, HD), HD)
        kk = kx[1:17, :, cols].reshape(ROWS, HD)
        vv = vx[1:17, :, cols].reshape(ROWS, HD)
        st = lax.dot_general(kk, gq[:, cols], NT, preferred_element_type=F32)
        m = jnp.max(st, axis=0, keepdims=True)
        p = jnp.exp2((st - m) * SCALE2)
        l = jnp.sum(p, axis=0, keepdims=True)
        part[h, 0:HD, :] = lax.dot_general(vv, p.astype(BF), TN, preferred_element_type=F32)
        row = lax.broadcasted_iota(jnp.int32, (8, HD), 0)
        part[h, HD:HD + 8, :] = jnp.where(row == 0, m, jnp.where(row == 1, l, 0.0))
        return carry

    lax.fori_loop(0, 8, glob, 0)
    for cp in to_s:
        cp.start()
        cp.wait()

    red1 = []
    for i, (dx, dc) in enumerate(row_peers):
        tgt = ((x + dx) % 4) * 2 + (c + dc) % 2
        red1.append(go(remote(part.at[tgt], r1.at[xc], r1_s.at[i], r1_r.at[i], at(dx=dx, dc=dc))))

    def forward(g):
        a, b, d, e, f, h = g
        a.wait_recv()
        go(f)
        b.wait_recv()
        go(h)

    forward(agk)
    forward(agv)
    for g in (agk, agv):
        a, b, d, e, f, h = g
        for cp in (d, e, f, h):
            cp.wait_recv()

    @pl.when(is00)
    def _():
        for dx in (1, 3, 2):
            gcopy(kag.at[0, pl.ds(0, 2)], gk, 3, dx, at(dx=dx)).start()
        gcopy(kag.at[0, pl.ds(0, 2)], gk, 4, 0, mate).start()
        gk[...] = kag[0, 0:2]

    first = jnp.logical_and(z == 0, c == 0)

    @pl.when(first)
    def _():
        for dz in (1, 3, 2):
            gcopy(vag.at[0, pl.ds(0, 2)], gv, 5, dz, at(dz=dz)).start()
        gcopy(vag.at[0, pl.ds(0, 2)], gv, 6, 0, mate).start()
        gv[...] = vag[0, 0:2]

    def stage(ch, j):
        cols = pl.ds(ch * CW, CW)

        def put(n, carry):
            i, t = n // 8, n % 8
            stk[j, i, t] = kag[t // 2, sqk[i, 0, t], :, cols]
            stv[j, i, t] = vag[t // 2, sqv[i, 0, t], :, cols]
            return carry

        lax.fori_loop(0, 64, put, 0)
        rk, rv = rks[ch], rvs[ch]

        def keep(t, carry):
            rk[xc * 8 + t] = stk[j, xc, t]
            rv[zc * 8 + t] = stv[j, zc, t]
            return carry

        lax.fori_loop(0, 8, keep, 0)

    def exchange(ch, j):
        rk, rv = rks[ch], rvs[ch]
        out = []
        for i, (dx, dc) in enumerate(row_peers):
            tgt = ((x + dx) % 4) * 2 + (c + dc) % 2
            out.append(remote(stk.at[j, tgt], rk.at[pl.ds(xc * 8, 8)], a2_s.at[ch, 0, i], a2_r.at[ch, 0, i], at(dx=dx, dc=dc)))
            tgt = ((z + dx) % 4) * 2 + (c + dc) % 2
            out.append(remote(stv.at[j, tgt], rv.at[pl.ds(zc * 8, 8)], a2_s.at[ch, 1, i], a2_r.at[ch, 1, i], at(dz=dx, dc=dc)))
        for cp in out:
            cp.start()
        return out

    def attend(ch):
        rk, rv = rks[ch], rvs[ch]

        def block(b, carry):
            r0 = pl.multiple_of(b * BLK, BLK)
            lane = lax.broadcasted_iota(jnp.int32, (1, 512), 1)
            no_left = jnp.logical_and(s == 0, b == 0)
            no_right = jnp.logical_and(s == 31, b == 15)
            low = jnp.where(no_left, BLK, 0)
            cut = jnp.where(no_right, 2 * BLK, 3 * BLK)
            gone = jnp.logical_or(lane < low, jnp.logical_and(lane >= cut, lane < 3 * BLK))
            bias = jnp.where(gone, -1e30, 0.0)
            for hh in range(HPC):
                c0 = ch * CW + hh * HD
                q = qv[pl.ds(r0, BLK), c0:c0 + HD]
                ks = [kx[pl.ds(b, 3), :, c0:c0 + HD].reshape(3 * BLK, HD)]
                ks += [rk[kidx[b * 3 + r], :, hh * HD:(hh + 1) * HD] for r in range(3)]
                ks += [gk[:, :, c0:c0 + HD].reshape(GLOB, HD)]
                vs = [vx[pl.ds(b, 3), :, c0:c0 + HD].reshape(3 * BLK, HD)]
                vs += [rv[vidx[b * 3 + r], :, hh * HD:(hh + 1) * HD] for r in range(3)]
                vs += [gv[:, :, c0:c0 + HD].reshape(GLOB, HD)]
                sc = lax.dot_general(q, jnp.concatenate(ks, axis=0), NT, preferred_element_type=F32)
                sc = sc + bias
                m = jnp.max(sc, axis=1, keepdims=True)
                p = jnp.exp2((sc - m) * SCALE2)
                l = jnp.sum(p, axis=1, keepdims=True)
                o = jnp.dot(p.astype(BF), jnp.concatenate(vs, axis=0), preferred_element_type=F32)
                att[pl.ds(r0, BLK), c0:c0 + HD] = (o / l).astype(BF)
            return carry

        lax.fori_loop(0, 16, block, 0)

    ysends = []

    def yparts(ch):
        out = []
        for dy in (1, 3, 2):
            tgt = (y + dy) % 4
            for hf in range(2):
                cp = remote(
                    att.at[pl.ds(tgt * 256 + hf * GLOB, GLOB), pl.ds(ch * CW, CW)],
                    att_out.at[pl.ds(hf * GLOB, GLOB), pl.ds(y * WIDTH + ch * CW, CW)],
                    y_s.at[ch, hf, dy], y_r.at[ch, hf, dy], at(dy=dy),
                )
                skip_send = jnp.logical_and(s == 0, tgt == 0) if hf == 0 else None
                skip_recv = root if hf == 0 else None
                out.append((cp, skip_send, skip_recv))
        for hf in range(2):
            cp = pltpu.make_async_copy(
                att.at[pl.ds(y * 256 + hf * GLOB, GLOB), pl.ds(ch * CW, CW)],
                att_out.at[pl.ds(hf * GLOB, GLOB), pl.ds(y * WIDTH + ch * CW, CW)],
                y_s.at[ch, hf, 0],
            )
            out.append((cp, root if hf == 0 else None, None))
        return out

    def unless(cond, f):
        if cond is None:
            f()
        else:
            pl.when(jnp.logical_not(cond))(f)

    def ysend(ch):
        out = yparts(ch)
        for cp, skip, _ in out:
            unless(skip, cp.start)
        ysends.append(out)

    def weight_forward():
        a, b, d, e, f, g = agw
        a.wait_recv()
        go(f)
        b.wait_recv()
        go(g)

    def wmate(n, m, p):
        return go(remote(wview(m, p), wview(m, p), wd_s.at[n], wd_r.at[n], mate))

    stage(0, 0)
    sent = [exchange(0, 0)]
    stage(1, 1)
    sent.append(exchange(1, 1))
    weight_forward()
    left, right, far = (y + 3) % 4, (y + 1) % 4, (y + 2) % 4
    wm = [wmate(0, left, 0), wmate(1, right, 1)]

    for cp in edges:
        cp.wait_recv()

    @pl.when(jnp.logical_and(c == 0, x != 0))
    def _():
        gcopy(gk, gk, 3, 0, at()).wait_recv()
        gcopy(gk, gk, 4, 0, mate).start()

    @pl.when(jnp.logical_and(c == 0, z != 0))
    def _():
        gcopy(gv, gv, 5, 0, at()).wait_recv()
        gcopy(gv, gv, 6, 0, mate).start()

    @pl.when(c == 1)
    def _():
        gcopy(gk, gk, 4, 0, at()).wait_recv()
        gcopy(gv, gv, 6, 0, at()).wait_recv()

    def arrived(ch):
        for cp in sent[ch]:
            cp.wait_recv()

    def merge(buf, n, dst):
        m = buf[0, HD:HD + 1, :]
        for i in range(1, n):
            m = jnp.maximum(m, buf[i, HD:HD + 1, :])
        l = jnp.zeros((1, HD), F32)
        a = jnp.zeros((HD, HD), F32)
        for i in range(n):
            f = jnp.exp2((buf[i, HD:HD + 1, :] - m) * SCALE2)
            l = l + buf[i, HD + 1:HD + 2, :] * f
            a = a + buf[i, 0:HD, :] * f
        dst(m, l, a)

    arrived(0)
    attend(0)
    for cp in sent[0]:
        cp.wait_send()
    stage(2, 0)
    sent.append(exchange(2, 0))
    ysend(0)

    for cp in red1:
        cp.wait_recv()
    r1[xc] = part[xc]

    def to_comb(m, l, a):
        comb[0:HD, :] = a
        row = lax.broadcasted_iota(jnp.int32, (8, HD), 0)
        comb[HD:HD + 8, :] = jnp.where(row == 0, m, jnp.where(row == 1, l, 0.0))

    merge(r1, 8, to_comb)

    arrived(1)
    attend(1)
    for dz in (1, 2, 3):
        @pl.when(z == dz)
        def _(dz=dz):
            remote(comb, r2.at[dz], r2_s.at[dz], r2_r.at[dz], at(dz=4 - dz)).start()

    for cp in sent[1]:
        cp.wait_send()
    stage(3, 1)
    sent.append(exchange(3, 1))
    ysend(1)
    a, b, d, e, f, g = agw
    d.wait_recv()
    e.wait_recv()
    wm += [wmate(2, left, 1), wmate(3, right, 0)]

    def gplace(yy, hh):
        return att_out.at[pl.ds(0, GLOB), pl.ds(yy * WIDTH + hh * HD, HD)]

    @pl.when(z == 0)
    def _():
        for dz in (1, 2, 3):
            remote(comb, r2.at[dz], r2_s.at[dz], r2_r.at[dz], at()).wait_recv()
        r2[0] = comb[...]

        def finish(m, l, a):
            gout[...] = jnp.transpose(a / l).astype(BF)

        merge(r2, 4, finish)

    arrived(2)
    attend(2)

    @pl.when(z == 0)
    def _():
        @pl.when(root)
        def _():
            pltpu.make_async_copy(gout, gplace(0, 0), r3_r.at[0]).start()

        @pl.when(jnp.logical_not(root))
        def _():
            remote(gout, gplace(y, xc), r3_s, r3_r.at[y * 8 + xc], (0, 0)).start()

    ysend(2)
    f.wait_recv()
    g.wait_recv()
    wm += [wmate(4, far, 0), wmate(5, far, 1)]

    arrived(3)
    attend(3)
    ysend(3)

    for out in ysends:
        for i, (cp, skip_send, skip_recv) in enumerate(out):
            if i < 6:
                unless(skip_send, cp.wait_send)
                unless(skip_recv, cp.wait_recv)
            else:
                unless(skip_send, cp.wait)

    @pl.when(z == 0)
    def _():
        @pl.when(root)
        def _():
            pltpu.make_async_copy(gout, gplace(0, 0), r3_r.at[0]).wait()
            for n in range(1, 32):
                remote(gout, gplace(n // 8, n % 8), r3_s, r3_r.at[n], (0, 0)).wait_recv()

        @pl.when(jnp.logical_not(root))
        def _():
            remote(gout, gplace(y, xc), r3_s, r3_r.at[y * 8 + xc], (0, 0)).wait_send()

    for dz in (1, 2, 3):
        @pl.when(z == dz)
        def _(dz=dz):
            remote(comb, r2.at[dz], r2_s.at[dz], r2_r.at[dz], at(dz=4 - dz)).wait_send()

    wown.wait_recv()
    for cp in wm:
        cp.wait_recv()
    for cp in late:
        cp.wait_send()
    for ch in (2, 3):
        for cp in sent[ch]:
            cp.wait_send()

    @pl.when(s == 0)
    def _():
        for dz in (1, 3, 2):
            gcopy(q_top, gq, 0, dz, at(dz=dz)).wait_send()

    @pl.when(is00)
    def _():
        for dx in (1, 3, 2):
            gcopy(gq, gq, 1, dx, at(dx=dx)).wait_send()
            gcopy(gk, gk, 3, dx, at(dx=dx)).wait_send()

    @pl.when(first)
    def _():
        for dz in (1, 3, 2):
            gcopy(gv, gv, 5, dz, at(dz=dz)).wait_send()

    @pl.when(c == 0)
    def _():
        gcopy(gq, gq, 2, 0, mate).wait_send()
        gcopy(gk, gk, 4, 0, mate).wait_send()
        gcopy(gv, gv, 6, 0, mate).wait_send()


def local(queries, key_rows, value_rows, random_owner, random_local, output_weight):
    reqk, reqv, kidx, vidx = tables(random_owner, random_local)
    smem = pl.BlockSpec(memory_space=pltpu.SMEM)
    vmem = pl.BlockSpec(memory_space=pltpu.VMEM)
    hbm = pl.BlockSpec(memory_space=pl.ANY)
    dma = pltpu.SemaphoreType.DMA
    scratch = [
        pltpu.VMEM((4, 16, BLK, WIDTH), BF),
        pltpu.VMEM((4, 16, BLK, WIDTH), BF),
        pltpu.VMEM((18, BLK, WIDTH), BF),
        pltpu.VMEM((18, BLK, WIDTH), BF),
        pltpu.VMEM((ROWS, WIDTH), BF),
        pltpu.VMEM((2, 8, 8, BLK, CW), BF),
        pltpu.VMEM((2, 8, 8, BLK, CW), BF),
    ]
    scratch += [pltpu.VMEM((64, BLK, CW), BF) for _ in range(8)]
    scratch += [pltpu.VMEM((GLOB, WIDTH), BF)]
    scratch += [pltpu.VMEM((2, BLK, WIDTH), BF) for _ in range(2)]
    scratch += [
        pltpu.VMEM((ROWS, WIDTH), BF),
        pltpu.VMEM((8, HD + 8, HD), F32),
        pltpu.VMEM((8, HD + 8, HD), F32),
        pltpu.VMEM((4, HD + 8, HD), F32),
        pltpu.VMEM((HD + 8, HD), F32),
        pltpu.VMEM((GLOB, HD), BF),
        pltpu.VMEM((8, 1, 128), jnp.int32),
        pltpu.VMEM((8, 1, 128), jnp.int32),
        pltpu.SMEM((8, 1, 128), jnp.int32),
        pltpu.SMEM((8, 1, 128), jnp.int32),
        dma((7,)),
        dma((2, 7)), dma((2, 7)),
        dma((2, 2)), dma((2, 2)),
        dma((2, 6)), dma((2, 6)),
        dma((1, 6)), dma((1, 6)),
        dma((7,)), dma((7,)),
        dma((CHUNKS, 2, 7)), dma((CHUNKS, 2, 7)),
        dma((7, 4)), dma((7,)),
        dma((CHUNKS, 2, 4)), dma((CHUNKS, 2, 4)),
        dma((7,)), dma((7,)),
        dma((4,)), dma((4,)),
        dma, dma((32,)),
    ]
    att, wfull = pl.pallas_call(
        main_kernel,
        out_shape=[
            jax.ShapeDtypeStruct((256, 4096), BF),
            jax.ShapeDtypeStruct((4096, 4096), BF),
        ],
        in_specs=[smem, smem, vmem, vmem, hbm, hbm, hbm, hbm],
        out_specs=[hbm, hbm],
        scratch_shapes=scratch,
        compiler_params=pltpu.CompilerParams(
            collective_id=0, has_side_effects=True, vmem_limit_bytes=63 * 2**20
        ),
        name="exchange_attend",
    )(
        kidx, vidx, reqk, reqv, queries, key_rows.reshape(16, BLK, WIDTH),
        value_rows.reshape(16, BLK, WIDTH), output_weight,
    )
    return jnp.dot(att, wfull, preferred_element_type=F32).astype(BF)


def solution(mesh):
    return jax.shard_map(
        local,
        mesh=mesh,
        in_specs=(
            P("seq", "head"),
            P("seq", "head"),
            P("seq", "head"),
            P("seq", None),
            P("seq", None),
            P("head", None),
        ),
        out_specs=P(("seq", "head"), None),
        check_vma=False,
    )
```

time: 733 us -> 248 us (0.34)
  blocking collectives: 271 us -> 0 us
  Pallas kernels: 0 us -> 228 us
  local copies, waits for them, and re-layouts: 168 us -> 2.7 us
  waiting for transfers between devices: 148 us -> 0 us
  other arithmetic: 63 us -> 0 us
  matrix products: 50.1 us -> 16.6 us
  starting transfers between devices: 15.3 us -> 0 us
  between operations: 13.4 us -> 0.02 us
    pallas_call x0 -> x2, Pallas kernels: none -> 228 us  [the longest x1 224 us: local(): pl.pallas_call(main_kernel, out_shape=[jax.ShapeDtypeStruct((256, 4096),...]
    all_to_all x2 -> x0, blocking collectives: 159 us -> none  [the longest x1 143 us: local(): lax.all_to_all(sent_values, SEQ, split_axis=0, concat_axis=0, tiled=True)]
    reduce_scatter x1 -> x0, waiting for transfers between devices: 146 us -> none  [local(): lax.psum_scatter(jnp.dot(attention, output_weight, preferred_element_type...]
    all_gather x6 -> x0, blocking collectives: 113 us -> none  [combined_by_axis(): pieces = jax.tree.map(lambda part: lax.all_gather(part, axis), array)]
    while x24 -> x0, local copies, waits for them, and re-layouts: 69.9 us -> none
    dot_general x7 -> x1, matrix products: 50.1 us -> 16.6 us  [local(): return jnp.dot(att, wfull, preferred_element_type=F32).astype(BF)]
    gather x4 -> x0, local copies, waits for them, and re-layouts: 29.8 us -> none  [the longest x1 8.49 us: local(): jnp.take(got_keys.reshape(-1, BLOCK, width_here), flat_slots, axis=0)]
    all_gather x1 -> x0, local copies, waits for them, and re-layouts: 29.5 us -> none  [broadcast(): lax.all_gather(array, axis)]
  transfers between devices with their start and end apart: 8 -> 0, of which waited for: 2 -> 0; matrix products, arithmetic and copies ran while one was open for 34% -> 0% of each run, Pallas kernels for 0% -> 0%
where the time goes in v1:
time: 248 us; the launch traced here: 247 us
  Pallas kernels  228 us (92%)
  matrix products  16.6 us (7%)
  local copies, waits for them, and re-layouts  2.7 us (1%)
    pallas_call x1, Pallas kernels, local(): pl.pallas_call(main_kernel, out_shape=[jax.ShapeDtypeStruct((256, 4096),...  224 us
    dot_general x1, matrix products, local(): return jnp.dot(att, wfull, preferred_element_type=F32).astype(BF)  16.6 us

profile of v1, /device:TPU:1, one launch (start us, length us, event | category | flops | bytes accessed | tf_op | source)
XLA Modules:
  0.0 247.4 jit_solution(6451375006462383450)
XLA Ops:
  0.0 1.4 copy.7.owner
  1.4 1.3 copy.8.place
  2.7 4.4 %tables.1 = (s32[8,1,128]{2,1,0:T(1,128)}, s32[8,1,128]{2,1,0:T(1,128)}, s32[48]{0:T(128)}, s32[48]{0:T(128)}) custom-call(s32[16,3]{1,0:T(8,128)} %copy.7.owner, s32[16,3]{1,0:T(8,128)} %copy.8.place), custom_call_target="tpu_custom_call" | custom-call | tf_op jit(solution)/shard_map/tables/pallas_call | solution.py:58
  7.1 223.7 %exchange_attend.1 = (bf16[256,4096]{1,0:T(8,128)(2,1)}, bf16[4096,4096]{1,0:T(8,128)(2,1)}) custom-call(s32[48]{0:T(128)} %get-tuple-element.11.kidx, s32[48]{0:T(128)} %get-tuple-element.12.vidx, s32[8,1,128]{2,1,0:T(1,128)} %get-tuple-element.13.reqk, s32[8,1,128]{2,1,0:T(1,128)} %get-tuple-element.14.reqv, bf16[1024,1024]{1,0:T(8,128)(2,1)} %q_hbm.1, ...), custom_call_target="tpu_custom_call" | custom-call | tf_op jit(solution)/shard_map/exchange_attend/pallas_call | solution.py:614
  230.8 16.6 %convolution_convert_fusion = bf16[256,4096]{1,0:T(8,128)(2,1)} fusion(bf16[256,4096]{1,0:T(8,128)(2,1)} %get-tuple-element.15, bf16[4096,4096]{1,0:T(8,128)(2,1)} %get-tuple-element.16), kind=kOutput, calls=%fused_computation | convolution fusion | flops 8590983168 | bytes 37748736 | tf_op jit(solution)/shard_map/dot_general | solution.py:631

commit v2 on v1

v2 whole, which is shorter than its diff:
```python
import math

import jax
import jax.numpy as jnp
from jax import lax
from jax.experimental import pallas as pl
from jax.experimental.pallas import tpu as pltpu
from jax.sharding import PartitionSpec as P

MESH = pl.DeviceIdType.MESH
HD = 128
BLK = 64
GLOB = 128
RANDOM = 3
UNITS = 2
ROWS = 1024
WIDTH = 1024
HEADS_OF = ((0, 2), (2, 2), (4, 2), (6, 1), (7, 1))
CHUNKS = len(HEADS_OF)
SCALE2 = HD ** (-0.5) * math.log2(math.e)
BF = jnp.bfloat16
F32 = jnp.float32
NT = (((1,), (1,)), ((), ()))
TN = (((0,), (0,)), ((), ()))


def main_kernel(
    owner, place, q_hbm, k_hbm, v_hbm, w_hbm,
    out_hbm, wfull,
    kag, vag, kx, vx, qv, stk0, stv0, stk1, stv1, stk2, stv2, *rest,
):
    rks, rvs, rest = rest[:CHUNKS], rest[CHUNKS:2 * CHUNKS], rest[2 * CHUNKS:]
    (
        gq, gk, gv, att, atts, acc, outv, part, pml, r1, m1, r2, comb, gout, reqk, reqv, rqk, rqv, sqk, sqv, kidx, vidx,
        loc, rq_s, rq_r, ed_s, ed_r, ag_s, ag_r, w_s, w_r, wd_s, wd_r,
        a2_s, a2_r, g_s, g_r, y_s, y_r, r1_s, r1_r, r2_s, r2_r, r3_s, r3_r, pf, ob,
    ) = rest
    stages = ((stk0, stv0), (stk1, stv1), (stk0, stv0), (stk1, stv1), (stk2, stv2))
    s = lax.axis_index("seq")
    y = lax.axis_index("head")
    z, x, c = s // 8, (s // 2) % 4, s % 2
    xc, zc = x * 2 + c, z * 2 + c

    def at(dz=0, dx=0, dc=0, dy=0):
        return ((((z + dz) % 4) * 4 + (x + dx) % 4) * 2 + (c + dc) % 2, (y + dy) % 4)

    def remote(src, dst, ss, rs, dev):
        return pltpu.make_async_remote_copy(
            src_ref=src, dst_ref=dst, send_sem=ss, recv_sem=rs, device_id=dev, device_id_type=MESH
        )

    def unless(cond, f):
        if cond is None:
            f()
        else:
            pl.when(jnp.logical_not(cond))(f)

    nxt, prv = ((s + 1) % 32, y), ((s + 31) % 32, y)
    row_peers = [(dx, dc) for dx in (1, 3, 2, 0) for dc in (0, 1) if (dx, dc) != (0, 0)]

    own = [
        pltpu.make_async_copy(k_hbm, kag.at[z], loc.at[0]),
        pltpu.make_async_copy(v_hbm, vag.at[x], loc.at[1]),
        pltpu.make_async_copy(k_hbm, kx.at[pl.ds(1, 16)], loc.at[2]),
        pltpu.make_async_copy(v_hbm, vx.at[pl.ds(1, 16)], loc.at[3]),
        pltpu.make_async_copy(q_hbm, qv, loc.at[4]),
    ]
    for cp in own:
        cp.start()

    bar = pltpu.get_barrier_semaphore()
    peers = [at(dx=dx, dc=dc) for dx, dc in row_peers]
    peers += [at(dz=dz, dc=dc) for dz in (1, 2, 3) for dc in (0, 1)]
    peers += [at(dy=dy) for dy in (1, 2, 3)]
    peers += [nxt, prv]
    for dev in peers:
        pl.semaphore_signal(bar, inc=1, device_id=dev, device_id_type=MESH)
    root = jnp.logical_and(s == 0, y == 0)

    @pl.when(z == 0)
    def _():
        @pl.when(jnp.logical_not(root))
        def _():
            pl.semaphore_signal(bar, inc=1, device_id=(0, 0), device_id_type=MESH)

    @pl.when(root)
    def _():
        for ss in range(8):
            for yy in range(4):
                if (ss, yy) != (0, 0):
                    pl.semaphore_signal(bar, inc=1, device_id=(ss, yy), device_id_type=MESH)
        pl.semaphore_wait(bar, len(peers) + 31)

    @pl.when(jnp.logical_not(root))
    def _():
        @pl.when(z == 0)
        def _():
            pl.semaphore_wait(bar, len(peers) + 1)

        @pl.when(z != 0)
        def _():
            pl.semaphore_wait(bar, len(peers))

    late = []

    def go(cp):
        cp.start()
        late.append(cp)
        return cp

    is00 = jnp.logical_and(x == 0, c == 0)
    mate = at(dc=1)

    def gcopy(src, dst, n, i, dev):
        return remote(src, dst, g_s.at[n, i], g_r.at[n], dev)

    q_top = q_hbm.at[pl.ds(0, GLOB)]
    q_root = pltpu.make_async_copy(q_top, gq, g_r.at[0])

    @pl.when(s == 0)
    def _():
        q_root.start()
        for dz in (1, 3, 2):
            gcopy(q_top, gq, 0, dz, at(dz=dz)).start()

    def gather(n, own_view, view, up, down, me, ss, rs):
        a = remote(own_view(0), view(me, 0), ss.at[n, 0], rs.at[n, 0], up)
        b = remote(own_view(1), view(me, 1), ss.at[n, 1], rs.at[n, 1], down)
        d = remote(own_view(1), view(me, 1), ss.at[n, 2], rs.at[n, 2], up)
        e = remote(own_view(0), view(me, 0), ss.at[n, 3], rs.at[n, 3], down)
        before, after = (me + 3) % 4, (me + 1) % 4
        f = remote(view(before, 0), view(before, 0), ss.at[n, 4], rs.at[n, 4], up)
        g = remote(view(after, 1), view(after, 1), ss.at[n, 5], rs.at[n, 5], down)
        return a, b, d, e, f, g

    agk = gather(
        0, lambda p: k_hbm.at[pl.ds(p * 8, 8)],
        lambda m, p: kag.at[m, pl.ds(p * 8, 8)], at(dz=1), at(dz=3), z, ag_s, ag_r,
    )
    agv = gather(
        1, lambda p: v_hbm.at[pl.ds(p * 8, 8)],
        lambda m, p: vag.at[m, pl.ds(p * 8, 8)], at(dx=1), at(dx=3), x, ag_s, ag_r,
    )

    def wview(m, p):
        return wfull.at[pl.ds(m * 16 + c * 8 + p * 4, 4)]

    agw = gather(
        0, lambda p: w_hbm.at[pl.ds(c * 8 + p * 4, 4)],
        wview, at(dy=1), at(dy=3), y, w_s, w_r,
    )
    for n in range(4):
        for g in (agk, agv, agw):
            g[n].start()

    edges = []
    for i, (hbm, ext) in enumerate(((k_hbm, kx), (v_hbm, vx))):
        edges.append(go(remote(hbm.at[0], ext.at[17], ed_s.at[i, 0], ed_r.at[i, 0], prv)))
        edges.append(go(remote(hbm.at[15], ext.at[0], ed_s.at[i, 1], ed_r.at[i, 1], nxt)))

    wown = go(remote(w_hbm, wfull.at[pl.ds(y * 16, 16)], wd_s.at[6], wd_r.at[6], mate))

    @pl.when(is00)
    def _():
        @pl.when(s == 0)
        def _():
            q_root.wait()

        @pl.when(s != 0)
        def _():
            gcopy(q_top, gq, 0, 0, at()).wait_recv()

        for dx in (1, 3, 2):
            gcopy(gq, gq, 1, dx, at(dx=dx)).start()

    reqk[...] = jnp.zeros((8, 1, 128), jnp.int32)
    reqv[...] = jnp.zeros((8, 1, 128), jnp.int32)
    lanes = lax.broadcasted_iota(jnp.int32, (1, 128), 1)

    def serve(o, carry):
        def look(b, st):
            n, p0, p1 = st
            for r in range(RANDOM):
                hit = owner[r, b] == o
                here = place[r, b]
                p0 = jnp.where(jnp.logical_and(hit, n == 0), here, p0)
                p1 = jnp.where(jnp.logical_and(hit, n == 1), here, p1)
                n = n + jnp.where(hit, 1, 0)
            return n, p0, p1

        zero = jnp.int32(0)
        _, p0, p1 = lax.fori_loop(0, 16, look, (zero, zero, zero))
        oz, ox, oc = o // 8, (o // 2) % 4, o % 2

        def row(old, t):
            return jnp.where(lanes == t, p0, jnp.where(lanes == t + 1, p1, old))

        reqk[ox * 2 + oc] = row(reqk[ox * 2 + oc], oz * 2)
        reqv[oz * 2 + oc] = row(reqv[oz * 2 + oc], ox * 2)
        return carry

    lax.fori_loop(0, 32, serve, 0)

    def number(b, carry):
        for r in range(RANDOM):
            o = owner[r, b]

            def before(bb, n):
                for rr in range(RANDOM):
                    n = n + jnp.where(owner[rr, bb] == o, 1, 0)
                return n

            n = lax.fori_loop(0, b, before, jnp.int32(0))
            oz, ox, oc = o // 8, (o // 2) % 4, o % 2
            kidx[b * RANDOM + r] = (ox * 2 + oc) * 8 + oz * 2 + n
            vidx[b * RANDOM + r] = (oz * 2 + oc) * 8 + ox * 2 + n
        return carry

    lax.fori_loop(0, 16, number, 0)

    rq = []
    for i, (dx, dc) in enumerate(row_peers):
        tgt = ((x + dx) % 4) * 2 + (c + dc) % 2
        rq.append(go(remote(reqk.at[tgt], rqk.at[xc], rq_s.at[0, i], rq_r.at[0, i], at(dx=dx, dc=dc))))
        tgt = ((z + dx) % 4) * 2 + (c + dc) % 2
        rq.append(go(remote(reqv.at[tgt], rqv.at[zc], rq_s.at[1, i], rq_r.at[1, i], at(dz=dx, dc=dc))))

    def forward(g):
        g[0].wait_recv()
        g[4].start()
        g[1].wait_recv()
        g[5].start()

    forward(agk)
    forward(agv)
    for cp in own:
        cp.wait()

    @pl.when(c == 0)
    def _():
        @pl.when(x != 0)
        def _():
            gcopy(gq, gq, 1, 0, at()).wait_recv()

        gcopy(gq, gq, 2, 0, mate).start()

    @pl.when(c == 1)
    def _():
        gcopy(gq, gq, 2, 0, at()).wait_recv()

    left, right, far = (y + 3) % 4, (y + 1) % 4, (y + 2) % 4

    def wmate(n, m, p):
        return go(remote(wview(m, p), wview(m, p), wd_s.at[n], wd_r.at[n], mate))

    row8 = lax.broadcasted_iota(jnp.int32, (8, HD), 0)

    def max_total(m, l):
        return jnp.where(row8 == 0, m, jnp.where(row8 == 1, l, 0.0))

    def glob(h, carry):
        cols = pl.ds(pl.multiple_of(h * HD, HD), HD)
        kk = kx[1:17, :, cols].reshape(ROWS, HD)
        vv = vx[1:17, :, cols].reshape(ROWS, HD)
        st = lax.dot_general(kk, gq[:, cols], NT, preferred_element_type=F32)
        m = jnp.max(st, axis=0, keepdims=True)
        p = jnp.exp2((st - m) * SCALE2)
        l = jnp.sum(p, axis=0, keepdims=True)
        part[h] = lax.dot_general(vv, p.astype(BF), TN, preferred_element_type=F32).astype(BF)
        pml[h] = max_total(m, l)
        return carry

    lax.fori_loop(0, 8, glob, 0)

    forward(agw)
    wm = [wmate(0, left, 0), wmate(1, right, 1)]

    red1 = []
    for i, (dx, dc) in enumerate(row_peers):
        tgt = ((x + dx) % 4) * 2 + (c + dc) % 2
        red1.append(go(remote(part.at[tgt], r1.at[xc], r1_s.at[0, i], r1_r.at[0, i], at(dx=dx, dc=dc))))
        red1.append(go(remote(pml.at[tgt], m1.at[xc], r1_s.at[1, i], r1_r.at[1, i], at(dx=dx, dc=dc))))

    for cp in rq:
        cp.wait_recv()
    rqk[xc] = reqk[xc]
    rqv[zc] = reqv[zc]
    to_s = [pltpu.make_async_copy(rqk, sqk, loc.at[5]), pltpu.make_async_copy(rqv, sqv, loc.at[6])]
    for cp in to_s:
        cp.start()
    for cp in to_s:
        cp.wait()

    for g in (agk, agv):
        for cp in g[2:]:
            cp.wait_recv()

    @pl.when(is00)
    def _():
        for dx in (1, 3, 2):
            gcopy(kag.at[0, pl.ds(0, 2)], gk, 3, dx, at(dx=dx)).start()
        gcopy(kag.at[0, pl.ds(0, 2)], gk, 4, 0, mate).start()
        gk[...] = kag[0, 0:2]

    first = jnp.logical_and(z == 0, c == 0)

    @pl.when(first)
    def _():
        for dz in (1, 3, 2):
            gcopy(vag.at[0, pl.ds(0, 2)], gv, 5, dz, at(dz=dz)).start()
        gcopy(vag.at[0, pl.ds(0, 2)], gv, 6, 0, mate).start()
        gv[...] = vag[0, 0:2]

    def stage(ch):
        h0, nh = HEADS_OF[ch]
        cols, wide = pl.ds(h0 * HD, nh * HD), pl.ds(0, nh * HD)
        stk, stv = stages[ch]
        rk, rv = rks[ch], rvs[ch]

        def put(i, carry):
            for t in range(8):
                stk[i, t, :, wide] = kag[t // 2, sqk[i, 0, t], :, cols]
                stv[i, t, :, wide] = vag[t // 2, sqv[i, 0, t], :, cols]
            return carry

        lax.fori_loop(0, 8, put, 0)

        def keep(t, carry):
            rk[xc * 8 + t] = stk[xc, t, :, wide]
            rv[zc * 8 + t] = stv[zc, t, :, wide]
            return carry

        lax.fori_loop(0, 8, keep, 0)

    def exchange(ch):
        nh = HEADS_OF[ch][1]
        wide = pl.ds(0, nh * HD)
        stk, stv = stages[ch]
        rk, rv = rks[ch], rvs[ch]
        out = []
        for i, (dx, dc) in enumerate(row_peers):
            tgt = ((x + dx) % 4) * 2 + (c + dc) % 2
            out.append(remote(stk.at[tgt, :, :, wide], rk.at[pl.ds(xc * 8, 8)], a2_s.at[ch, 0, i], a2_r.at[ch, 0, i], at(dx=dx, dc=dc)))
            tgt = ((z + dx) % 4) * 2 + (c + dc) % 2
            out.append(remote(stv.at[tgt, :, :, wide], rv.at[pl.ds(zc * 8, 8)], a2_s.at[ch, 1, i], a2_r.at[ch, 1, i], at(dz=dx, dc=dc)))
        for cp in out:
            cp.start()
        return out

    def attend(ch, lo=0, hi=16):
        h0, nh = HEADS_OF[ch]
        rk, rv = rks[ch], rvs[ch]
        lane = lax.broadcasted_iota(jnp.int32, (1, 512), 1)

        def unit(b, bias, hh):
            c0 = (h0 + hh) * HD
            cc = slice(hh * HD, (hh + 1) * HD)
            q = qv[pl.ds(pl.multiple_of(b * BLK, BLK), BLK), c0:c0 + HD]
            ks = [kx[pl.ds(b, 3), :, c0:c0 + HD].reshape(3 * BLK, HD)]
            ks += [rk[kidx[b * RANDOM + r], :, cc] for r in range(RANDOM)]
            ks += [gk[:, :, c0:c0 + HD].reshape(GLOB, HD)]
            vs = [vx[pl.ds(b, 3), :, c0:c0 + HD].reshape(3 * BLK, HD)]
            vs += [rv[vidx[b * RANDOM + r], :, cc] for r in range(RANDOM)]
            vs += [gv[:, :, c0:c0 + HD].reshape(GLOB, HD)]
            sc = lax.dot_general(q, jnp.concatenate(ks, axis=0), NT, preferred_element_type=F32)
            sc = sc + bias
            m = jnp.max(sc, axis=1, keepdims=True)
            p = jnp.exp2((sc - m) * SCALE2)
            l = jnp.sum(p, axis=1, keepdims=True)
            o = jnp.dot(p.astype(BF), jnp.concatenate(vs, axis=0), preferred_element_type=F32)
            att[pl.ds(pl.multiple_of(b * BLK, BLK), BLK), c0:c0 + HD] = (o / l).astype(BF)

        per = UNITS // nh

        def block(bb, carry):
            for k in range(per):
                b = bb * per + k
                no_left = jnp.logical_and(s == 0, b == 0)
                no_right = jnp.logical_and(s == 31, b == 15)
                low = jnp.where(no_left, BLK, 0)
                cut = jnp.where(no_right, 2 * BLK, 3 * BLK)
                gone = jnp.logical_or(lane < low, jnp.logical_and(lane >= cut, lane < 3 * BLK))
                bias = jnp.where(gone, -1e30, 0.0)
                for hh in range(nh):
                    unit(b, bias, hh)
            return carry

        lax.fori_loop(lo // per, hi // per, block, 0)

    ysends = []

    def ysend(ch):
        h0, nh = HEADS_OF[ch]
        out = []
        for h in range(h0, h0 + nh):
            for dy in (1, 3, 2):
                tgt = (y + dy) % 4
                for hf in range(2):
                    cp = remote(
                        att.at[pl.ds(tgt * 256 + hf * GLOB, GLOB), pl.ds(h * HD, HD)],
                        atts.at[h, pl.ds(hf * GLOB, GLOB), pl.ds(y * HD, HD)],
                        y_s.at[h, hf, dy], y_r.at[h, hf, dy], at(dy=dy),
                    )
                    skip = jnp.logical_and(s == 0, tgt == 0) if hf == 0 else None
                    out.append((cp, skip, root if hf == 0 else None))
        for cp, skip, _ in out:
            unless(skip, cp.start)

        def keep(hf):
            rows = pl.ds(pl.multiple_of(y * 256 + hf * GLOB, GLOB), GLOB)
            for h in range(h0, h0 + nh):
                atts[h, hf * GLOB:(hf + 1) * GLOB, pl.ds(pl.multiple_of(y * HD, HD), HD)] = att[rows, h * HD:(h + 1) * HD]

        keep(1)
        unless(root, lambda: keep(0))
        ysends.append(out)

    def yrecv(ch):
        for cp, _, skip in ysends[ch]:
            unless(skip, cp.wait_recv)

    wbufs = ((kag, 0), (vag, 0), (kag, 0), (vag, 0), (vag, 8))

    def prefetch(ch):
        h0, nh = HEADS_OF[ch]
        buf, base = wbufs[ch]
        out = []
        for h in range(nh):
            for yy in range(4):
                for n in range(4):
                    out.append(pltpu.make_async_copy(
                        wfull.at[pl.ds(yy * 16 + (h0 + h) * 2, 2), :, pl.ds(n * WIDTH, WIDTH)],
                        buf.at[n, pl.ds(base + h * 8 + yy * 2, 2)], pf.at[h0 + h, yy * 4 + n],
                    ))
        for cp in out:
            cp.start(priority=1)
        return out

    def project(ch, copies):
        h0, nh = HEADS_OF[ch]
        buf, base = wbufs[ch]
        for cp in copies:
            cp.wait()

        def tile(j, carry):
            n, sub = j // 4, j % 4
            cols = pl.ds(pl.multiple_of(j * 256, 256), 256)
            w = buf[n, base:base + nh * 8, :, pl.ds(pl.multiple_of(sub * 256, 256), 256)].reshape(nh * 512, 256)
            rows = jnp.concatenate([atts[h] for h in range(h0, h0 + nh)], axis=1)
            t = jnp.dot(rows, w, preferred_element_type=F32)
            if ch == 0:
                acc[:, cols] = t
            elif ch < CHUNKS - 1:
                acc[:, cols] += t
            else:
                outv[:, cols] = (acc[:, cols] + t).astype(BF)
            return carry

        lax.fori_loop(0, 16, tile, 0)

    def merge(ml, part_of, n):
        m = ml(0)[0:1, :]
        for i in range(1, n):
            m = jnp.maximum(m, ml(i)[0:1, :])
        l = jnp.zeros((1, HD), F32)
        a = jnp.zeros((HD, HD), F32)
        for i in range(n):
            f = jnp.exp2((ml(i)[0:1, :] - m) * SCALE2)
            l = l + ml(i)[1:2, :] * f
            a = a + part_of(i) * f
        return m, l, a

    stage(0)
    sent = [exchange(0)]
    for cp in red1:
        cp.wait_recv()
    r1[xc] = part[xc]
    m1[xc] = pml[xc]
    m, l, a = merge(lambda i: m1[i], lambda i: r1[i].astype(F32), 8)
    comb[0:HD, :] = a
    comb[HD:HD + 8, :] = max_total(m, l)

    stage(1)
    for dz in (1, 2, 3):
        @pl.when(z == dz)
        def _(dz=dz):
            remote(comb, r2.at[dz], r2_s.at[dz], r2_r.at[dz], at(dz=4 - dz)).start()

    sent.append(exchange(1))
    stage(4)

    for cp in edges:
        cp.wait_recv()

    @pl.when(jnp.logical_and(c == 0, x != 0))
    def _():
        gcopy(gk, gk, 3, 0, at()).wait_recv()
        gcopy(gk, gk, 4, 0, mate).start()

    @pl.when(jnp.logical_and(c == 0, z != 0))
    def _():
        gcopy(gv, gv, 5, 0, at()).wait_recv()
        gcopy(gv, gv, 6, 0, mate).start()

    @pl.when(c == 1)
    def _():
        gcopy(gk, gk, 4, 0, at()).wait_recv()
        gcopy(gv, gv, 6, 0, at()).wait_recv()

    def arrived(ch):
        for cp in sent[ch]:
            cp.wait_recv()

    def refill(ch):
        for cp in sent[ch - 2]:
            cp.wait_send()
        stage(ch)
        sent.append(exchange(ch))

    agw[2].wait_recv()
    agw[3].wait_recv()
    wm += [wmate(2, left, 1), wmate(3, right, 0)]
    arrived(0)
    @pl.when(z == 0)
    def _():
        for dz in (1, 2, 3):
            remote(comb, r2.at[dz], r2_s.at[dz], r2_r.at[dz], at()).wait_recv()
        r2[0] = comb[...]
        _, l, a = merge(lambda i: r2[i, HD:HD + 8, :], lambda i: r2[i, 0:HD, :], 4)
        gout[...] = jnp.transpose(a / l).astype(BF)

    for cp in sent[0]:
        cp.wait_send()
    stage(2)
    def gfinal(yy, hh):
        return remote(gout, atts.at[hh, pl.ds(0, GLOB), pl.ds(yy * HD, HD)], r3_s, r3_r.at[yy * 8 + hh], (0, 0))

    @pl.when(z == 0)
    def _():
        @pl.when(root)
        def _():
            atts[0, 0:GLOB, 0:HD] = gout[...]

        unless(root, lambda: gfinal(y, xc).start())

    sent.append(exchange(2))
    attend(0)
    ysend(0)

    arrived(1)
    refill(3)
    sent.append(exchange(4))
    agw[4].wait_recv()
    agw[5].wait_recv()
    wm += [wmate(4, far, 0), wmate(5, far, 1)]
    attend(1)
    ysend(1)

    for g in (agk, agv):
        for cp in g:
            cp.wait_send()

    @pl.when(is00)
    def _():
        for dx in (1, 3, 2):
            gcopy(gk, gk, 3, dx, at(dx=dx)).wait_send()

    @pl.when(first)
    def _():
        for dz in (1, 3, 2):
            gcopy(gv, gv, 5, dz, at(dz=dz)).wait_send()

    @pl.when(c == 0)
    def _():
        gcopy(gk, gk, 4, 0, mate).wait_send()
        gcopy(gv, gv, 6, 0, mate).wait_send()

    wown.wait_recv()
    for cp in wm:
        cp.wait_recv()
    p0 = prefetch(0)
    p1 = prefetch(1)

    @pl.when(root)
    def _():
        for n in range(1, 32):
            gfinal(n // 8, n % 8).wait_recv()

    yrecv(0)
    project(0, p0)
    p2 = prefetch(2)
    yrecv(1)
    project(1, p1)
    p3 = prefetch(3)
    p4 = prefetch(4)
    arrived(2)
    attend(2)
    ysend(2)
    arrived(3)
    attend(3)
    ysend(3)
    yrecv(2)
    project(2, p2)
    arrived(4)
    attend(4)
    ysend(4)
    yrecv(3)
    project(3, p3 + p4)
    yrecv(4)
    project(4, [])
    done = pltpu.make_async_copy(outv, out_hbm, ob)
    done.start()

    for out in ysends:
        for cp, skip, _ in out:
            unless(skip, cp.wait_send)

    @pl.when(z == 0)
    def _():
        unless(root, lambda: gfinal(y, xc).wait_send())

    for dz in (1, 2, 3):
        @pl.when(z == dz)
        def _(dz=dz):
            remote(comb, r2.at[dz], r2_s.at[dz], r2_r.at[dz], at(dz=4 - dz)).wait_send()

    for cp in late:
        cp.wait_send()
    for cp in agw:
        cp.wait_send()
    for ch in (2, 3, 4):
        for cp in sent[ch]:
            cp.wait_send()

    @pl.when(s == 0)
    def _():
        for dz in (1, 3, 2):
            gcopy(q_top, gq, 0, dz, at(dz=dz)).wait_send()

    @pl.when(is00)
    def _():
        for dx in (1, 3, 2):
            gcopy(gq, gq, 1, dx, at(dx=dx)).wait_send()

    @pl.when(c == 0)
    def _():
        gcopy(gq, gq, 2, 0, mate).wait_send()

    done.wait()


def local(queries, key_rows, value_rows, random_owner, random_local, output_weight):
    smem = pl.BlockSpec(memory_space=pltpu.SMEM)
    hbm = pl.BlockSpec(memory_space=pl.ANY)
    dma = pltpu.SemaphoreType.DMA
    widest = max(nh for _, nh in HEADS_OF) * HD
    scratch = [
        pltpu.VMEM((4, 16, BLK, WIDTH), BF),
        pltpu.VMEM((4, 16, BLK, WIDTH), BF),
        pltpu.VMEM((18, BLK, WIDTH), BF),
        pltpu.VMEM((18, BLK, WIDTH), BF),
        pltpu.VMEM((ROWS, WIDTH), BF),
    ]
    scratch += [pltpu.VMEM((8, 8, BLK, widest), BF) for _ in range(4)]
    scratch += [pltpu.VMEM((8, 8, BLK, HEADS_OF[-1][1] * HD), BF) for _ in range(2)]
    scratch += [pltpu.VMEM((64, BLK, nh * HD), BF) for _ in range(2) for _, nh in HEADS_OF]
    scratch += [pltpu.VMEM((GLOB, WIDTH), BF)]
    scratch += [pltpu.VMEM((2, BLK, WIDTH), BF) for _ in range(2)]
    scratch += [
        pltpu.VMEM((ROWS, WIDTH), BF),
        pltpu.VMEM((8, 256, 512), BF),
        pltpu.VMEM((256, 4096), F32),
        pltpu.VMEM((256, 4096), BF),
        pltpu.VMEM((8, HD, HD), BF),
        pltpu.VMEM((8, 8, HD), F32),
        pltpu.VMEM((8, HD, HD), BF),
        pltpu.VMEM((8, 8, HD), F32),
        pltpu.VMEM((4, HD + 8, HD), F32),
        pltpu.VMEM((HD + 8, HD), F32),
        pltpu.VMEM((GLOB, HD), BF),
        pltpu.VMEM((8, 1, 128), jnp.int32),
        pltpu.VMEM((8, 1, 128), jnp.int32),
        pltpu.VMEM((8, 1, 128), jnp.int32),
        pltpu.VMEM((8, 1, 128), jnp.int32),
        pltpu.SMEM((8, 1, 128), jnp.int32),
        pltpu.SMEM((8, 1, 128), jnp.int32),
        pltpu.SMEM((16 * RANDOM,), jnp.int32),
        pltpu.SMEM((16 * RANDOM,), jnp.int32),
        dma((7,)),
        dma((2, 7)), dma((2, 7)),
        dma((2, 2)), dma((2, 2)),
        dma((2, 6)), dma((2, 6)),
        dma((1, 6)), dma((1, 6)),
        dma((7,)), dma((7,)),
        dma((CHUNKS, 2, 7)), dma((CHUNKS, 2, 7)),
        dma((7, 4)), dma((7,)),
        dma((8, 2, 4)), dma((8, 2, 4)),
        dma((2, 7)), dma((2, 7)),
        dma((4,)), dma((4,)),
        dma, dma((32,)),
        dma((8, 16)), dma,
    ]
    out, _ = pl.pallas_call(
        main_kernel,
        out_shape=[
            jax.ShapeDtypeStruct((256, 4096), BF),
            jax.ShapeDtypeStruct((64, BLK, 4096), BF),
        ],
        in_specs=[smem, smem, hbm, hbm, hbm, hbm],
        out_specs=[hbm, hbm],
        scratch_shapes=scratch,
        compiler_params=pltpu.CompilerParams(
            collective_id=0, has_side_effects=True, vmem_limit_bytes=67043328
        ),
        name="bigbird_layer",
    )(
        random_owner.T, random_local.T, queries, key_rows.reshape(16, BLK, WIDTH),
        value_rows.reshape(16, BLK, WIDTH), output_weight.reshape(16, BLK, 4096),
    )
    return out


def solution(mesh):
    return jax.shard_map(
        local,
        mesh=mesh,
        in_specs=(
            P("seq", "head"),
            P("seq", "head"),
            P("seq", "head"),
            P("seq", None),
            P("seq", None),
            P("head", None),
        ),
        out_specs=P(("seq", "head"), None),
        check_vma=False,
    )
```

time: 248 us -> 223 us (0.90); the launches traced: 247 us -> 219 us
  matrix products: 16.6 us -> 0 us
  Pallas kernels: 228 us -> 216 us
    dot_general x1 -> x0, matrix products: 16.6 us -> none  [local(): return jnp.dot(att, wfull, preferred_element_type=F32).astype(BF)]
    pallas_call x1, Pallas kernels: 224 us -> 216 us  [local(): pl.pallas_call(main_kernel, out_shape=[jax.ShapeDtypeStruct((256, 4096),...]
    pallas_call x1 -> x0, Pallas kernels: 4.42 us -> none  [tables(): pl.pallas_call(table_kernel, out_shape=[jax.ShapeDtypeStruct((8, 1, 128),...]
where the time goes in v2:
time: 223 us; the launch traced here: 219 us
  Pallas kernels  216 us (97%)
  local copies, waits for them, and re-layouts  3.13 us (1%)
    pallas_call x1, Pallas kernels, local(): pl.pallas_call(main_kernel, out_shape=[jax.ShapeDtypeStruct((256, 4096),...  216 us

profile of v2, /device:TPU:1, one launch (start us, length us, event | category | flops | bytes accessed | tf_op | source)
XLA Modules:
  0.0 218.7 jit_solution(10500923136181904176)
XLA Ops:
  0.0 215.6 %bigbird_layer.1 = (bf16[256,4096]{1,0:T(8,128)(2,1)}, bf16[64,64,4096]{2,1,0:T(8,128)(2,1)}) custom-call(s32[3,16]{1,0:T(4,128)} %bitcast.8, s32[3,16]{1,0:T(4,128)} %bitcast.9, bf16[1024,1024]{1,0:T(8,128)(2,1)} %q_hbm.1, bf16[16,64,1024]{2,1,0:T(8,128)(2,1)} %bitcast.6, bf16[16,64,1024]{2,1,0:T(8,128)(2,1)} %bitcast.7, bf16[16,64,4096]{2,1,0:T(8,128)(2,1)} %bitcast.5), custom_call_target="tpu_custom_call" | custom-call | tf_op jit(solution)/shard_map/bigbird_layer/pallas_call | solution.py:703
  215.6 3.1 %copy.8 = bf16[256,4096]{1,0:T(8,128)(2,1)} copy(bf16[256,4096]{1,0:T(8,128)(2,1)} %get-tuple-element.6) | data formatting | bytes 4194304

commit v3 on v2

--- a/solution.py
+++ b/solution.py
@@ -12,7 +12,7 @@
 BLK = 64
 GLOB = 128
 RANDOM = 3
-UNITS = 2
+UNITS = 8
 ROWS = 1024
 WIDTH = 1024
 HEADS_OF = ((0, 2), (2, 2), (4, 2), (6, 1), (7, 1))
@@ -438,25 +438,27 @@
 
     def project(ch, copies):
         h0, nh = HEADS_OF[ch]
+        if ch == 3:
+            nh = 2
         buf, base = wbufs[ch]
         for cp in copies:
             cp.wait()
 
         def tile(j, carry):
-            n, sub = j // 4, j % 4
-            cols = pl.ds(pl.multiple_of(j * 256, 256), 256)
-            w = buf[n, base:base + nh * 8, :, pl.ds(pl.multiple_of(sub * 256, 256), 256)].reshape(nh * 512, 256)
+            n, sub = j // 2, j % 2
+            cols = pl.ds(pl.multiple_of(j * 512, 512), 512)
+            w = buf[n, base:base + nh * 8, :, pl.ds(pl.multiple_of(sub * 512, 512), 512)].reshape(nh * 512, 512)
             rows = jnp.concatenate([atts[h] for h in range(h0, h0 + nh)], axis=1)
             t = jnp.dot(rows, w, preferred_element_type=F32)
             if ch == 0:
                 acc[:, cols] = t
-            elif ch < CHUNKS - 1:
+            elif ch < 3:
                 acc[:, cols] += t
             else:
                 outv[:, cols] = (acc[:, cols] + t).astype(BF)
             return carry
 
-        lax.fori_loop(0, 16, tile, 0)
+        lax.fori_loop(0, 8, tile, 0)
 
     def merge(ml, part_of, n):
         m = ml(0)[0:1, :]
@@ -589,25 +591,24 @@
     yrecv(0)
     project(0, p0)
     p2 = prefetch(2)
+    arrived(2)
+    attend(2)
+    ysend(2)
     yrecv(1)
     project(1, p1)
     p3 = prefetch(3)
     p4 = prefetch(4)
-    arrived(2)
-    attend(2)
-    ysend(2)
     arrived(3)
     attend(3)
     ysend(3)
-    yrecv(2)
-    project(2, p2)
     arrived(4)
     attend(4)
     ysend(4)
+    yrecv(2)
+    project(2, p2)
     yrecv(3)
+    yrecv(4)
     project(3, p3 + p4)
-    yrecv(4)
-    project(4, [])
     done = pltpu.make_async_copy(outv, out_hbm, ob)
     done.start()
 

time: 223 us -> 208 us (0.933); the launches traced: 219 us -> 206 us
  Pallas kernels: 216 us -> 203 us
    pallas_call x1, Pallas kernels: 216 us -> 203 us  [local(): pl.pallas_call(main_kernel, out_shape=[jax.ShapeDtypeStruct((256, 4096),...]
where the time goes in v3:
time: 208 us; the launch traced here: 206 us
  Pallas kernels  203 us (98%)
  local copies, waits for them, and re-layouts  3.13 us (2%)
    pallas_call x1, Pallas kernels, local(): pl.pallas_call(main_kernel, out_shape=[jax.ShapeDtypeStruct((256, 4096),...  203 us

profile of v3, /device:TPU:1, one launch (start us, length us, event | category | flops | bytes accessed | tf_op | source)
XLA Modules:
  0.0 206.3 jit_solution(4646873287536253194)
XLA Ops:
  0.0 203.2 %bigbird_layer.1 = (bf16[256,4096]{1,0:T(8,128)(2,1)}, bf16[64,64,4096]{2,1,0:T(8,128)(2,1)}) custom-call(s32[3,16]{1,0:T(4,128)} %bitcast.8, s32[3,16]{1,0:T(4,128)} %bitcast.9, bf16[1024,1024]{1,0:T(8,128)(2,1)} %q_hbm.1, bf16[16,64,1024]{2,1,0:T(8,128)(2,1)} %bitcast.6, bf16[16,64,1024]{2,1,0:T(8,128)(2,1)} %bitcast.7, bf16[16,64,4096]{2,1,0:T(8,128)(2,1)} %bitcast.5), custom_call_target="tpu_custom_call" | custom-call | tf_op jit(solution)/shard_map/bigbird_layer/pallas_call | solution.py:704
  203.2 3.1 %copy.8 = bf16[256,4096]{1,0:T(8,128)(2,1)} copy(bf16[256,4096]{1,0:T(8,128)(2,1)} %get-tuple-element.6) | data formatting | bytes 4194304

commit v4 on v3

--- a/solution.py
+++ b/solution.py
@@ -12,7 +12,7 @@
 BLK = 64
 GLOB = 128
 RANDOM = 3
-UNITS = 8
+UNITS = 16
 ROWS = 1024
 WIDTH = 1024
 HEADS_OF = ((0, 2), (2, 2), (4, 2), (6, 1), (7, 1))
@@ -456,6 +456,11 @@
                 acc[:, cols] += t
             else:
                 outv[:, cols] = (acc[:, cols] + t).astype(BF)
+
+                @pl.when(jnp.logical_and(j % 2 == 0, j > 0))
+                def _():
+                    wide = pl.ds(pl.multiple_of((n - 1) * WIDTH, WIDTH), WIDTH)
+                    pltpu.make_async_copy(outv.at[:, wide], out_hbm.at[:, wide], ob.at[n - 1]).start()
             return carry
 
         lax.fori_loop(0, 8, tile, 0)
@@ -609,8 +614,9 @@
     yrecv(3)
     yrecv(4)
     project(3, p3 + p4)
-    done = pltpu.make_async_copy(outv, out_hbm, ob)
-    done.start()
+
+    last = pl.ds(3 * WIDTH, WIDTH)
+    pltpu.make_async_copy(outv.at[:, last], out_hbm.at[:, last], ob.at[3]).start()
 
     for out in ysends:
         for cp, skip, _ in out:
@@ -647,7 +653,9 @@
     def _():
         gcopy(gq, gq, 2, 0, mate).wait_send()
 
-    done.wait()
+    for n in range(4):
+        wide = pl.ds(n * WIDTH, WIDTH)
+        pltpu.make_async_copy(outv.at[:, wide], out_hbm.at[:, wide], ob.at[n]).wait()
 
 
 def local(queries, key_rows, value_rows, random_owner, random_local, output_weight):
@@ -699,7 +707,7 @@
         dma((2, 7)), dma((2, 7)),
         dma((4,)), dma((4,)),
         dma, dma((32,)),
-        dma((8, 16)), dma,
+        dma((8, 16)), dma((4,)),
     ]
     out, _ = pl.pallas_call(
         main_kernel,

time: 208 us -> 207 us (level)
  no operation moved by 1% of the time
where the time goes in v4:
time: 207 us; the launch traced here: 206 us
  Pallas kernels  202 us (98%)
  local copies, waits for them, and re-layouts  3.13 us (2%)
    pallas_call x1, Pallas kernels, local(): pl.pallas_call(main_kernel, out_shape=[jax.ShapeDtypeStruct((256, 4096),...  202 us

profile of v4, /device:TPU:1, one launch (start us, length us, event | category | flops | bytes accessed | tf_op | source)
XLA Modules:
  0.0 205.5 jit_solution(9941225068123448658)
XLA Ops:
  0.0 202.4 %bigbird_layer.1 = (bf16[256,4096]{1,0:T(8,128)(2,1)}, bf16[64,64,4096]{2,1,0:T(8,128)(2,1)}) custom-call(s32[3,16]{1,0:T(4,128)} %bitcast.8, s32[3,16]{1,0:T(4,128)} %bitcast.9, bf16[1024,1024]{1,0:T(8,128)(2,1)} %q_hbm.1, bf16[16,64,1024]{2,1,0:T(8,128)(2,1)} %bitcast.6, bf16[16,64,1024]{2,1,0:T(8,128)(2,1)} %bitcast.7, bf16[16,64,4096]{2,1,0:T(8,128)(2,1)} %bitcast.5), custom_call_target="tpu_custom_call" | custom-call | tf_op jit(solution)/shard_map/bigbird_layer/pallas_call | solution.py:712
  202.4 3.1 %copy.8 = bf16[256,4096]{1,0:T(8,128)(2,1)} copy(bf16[256,4096]{1,0:T(8,128)(2,1)} %get-tuple-element.6) | data formatting | bytes 4194304
